TPU v7x, 32 devices: a 4x2x2 block of a 4x4x8 slice. The times are simulated.
32 devices in a mesh: dp: 4 (over y, z), tp: 8 (over x, core).
Axes of the slice: x: 4, y: 2, z: 2, core: 2. Of those that a mesh axis runs over, the one named last changes fastest.
The devices are a block of a 4x4x8 slice.
Arguments:
- hidden: bfloat16 [256, 5, 2048], P('dp'), parts along dimension 0
- norm_gain: float32 [2048], replicated
- w_head: bfloat16 [2048, 128256], P(None, 'tp')
- draft_probs: float32 [256, 4, 128256], P('dp', None, 'tp'), parts along dimension 0
- draft_tokens: int32 [256, 4], P('dp'), parts along dimension 0
- temperature: float32 [256], P('dp'), parts along dimension 0
Outputs:
- output 1: float32 [256, 4], P('dp'), parts along dimension 0
- output 2: float32 [256, 4], P('dp'), parts along dimension 0
- output 3: float32 [256, 4, 128256], P('dp', None, 'tp'), parts along dimension 0
- output 4: float32 [256], P('dp'), parts along dimension 0
There are 4 independent parts. A program takes and returns all parts, laid end to end along the dimension named above; an argument that names none is the same for every part.
All inputs are finite; a program needn't handle non-finite values.
Results may differ from a plain program's by a relative error of at most 0.001.
Values sent between devices are 32-bit elements.
A program may use at most 768 MiB of HBM per device.

v0:
```python
import jax
import jax.numpy as jnp
from jax import lax
from jax.sharding import PartitionSpec as P


def solution(mesh):
    def local_step(hidden, norm_gain, w_head, draft_probs, draft_tokens, value_a11):
        draft_len = draft_probs.shape[1]
        shard_vocab = w_head.shape[1]
        hidden_f32 = hidden.astype(jnp.float32)
        inv_rms = lax.rsqrt(jnp.mean(hidden_f32 * hidden_f32, axis=-1, keepdims=True) + 1e-5)
        normed = (hidden_f32 * inv_rms * norm_gain).astype(jnp.bfloat16)
        logits = jnp.einsum('cle,ew->clw', normed, w_head, preferred_element_type=jnp.float32)
        scaled = logits / value_a11[:, None, None]
        row_max = lax.pmax(jnp.max(scaled, axis=-1), 'tp')
        local_sum = jnp.sum(jnp.exp(scaled - row_max[:, :, None]), axis=-1)
        local_idx = draft_tokens - lax.axis_index('tp') * shard_vocab
        is_owned = (local_idx >= 0) & (local_idx < shard_vocab)
        safe_idx = jnp.clip(local_idx, 0, shard_vocab - 1)[:, :, None]
        tok_scaled = jnp.where(is_owned, jnp.take_along_axis(scaled[:, :draft_len], safe_idx, axis=-1)[:, :, 0], 0.0)
        tok_draft = jnp.where(is_owned, jnp.take_along_axis(draft_probs, safe_idx, axis=-1)[:, :, 0], 0.0)
        total_sum, tok_scaled, tok_draft = lax.psum((local_sum, tok_scaled, tok_draft), 'tp')
        row_lse = row_max + jnp.log(total_sum)
        draft_lse = row_lse[:, :draft_len]
        tok_target = jnp.exp(tok_scaled - draft_lse)
        accept = jnp.minimum(1.0, tok_target / tok_draft)
        excess = jnp.maximum(jnp.exp(scaled[:, :draft_len] - draft_lse[:, :, None]) - draft_probs, 0.0)
        norm_sum = lax.psum(jnp.sum(excess, axis=-1), 'tp')
        residual = excess / norm_sum[:, :, None]
        return accept, norm_sum, residual, row_lse[:, draft_len]

    return jax.shard_map(
        local_step,
        mesh=mesh,
        in_specs=(P('dp', None, None), P(), P(None, 'tp'), P('dp', None, 'tp'), P('dp', None), P('dp')),
        out_specs=(P('dp', None), P('dp', None), P('dp', None, 'tp'), P('dp')),
        check_vma=False,
    )
```

profile of v0, /device:TPU:81, one launch (start us, length us, event | category | flops | bytes accessed | tf_op | source)
XLA Modules:
  0.0 148.9 jit_solution(12625075280929576209)
XLA Ops:
  0.6 0.7 fusion.19
  1.4 1.7 %fusion.7 = f32[64,5]{0,1:T(8,128)S(1)} fusion(bf16[64,5,2048]{2,0,1:T(8,128)(2,1)} %param.8), kind=kLoop, calls=%fused_computation.12 | loop fusion | flops 1965760 | bytes 1312000 | tf_op jit(solution)/shard_map/reduce_sum | solution.py:12
  3.0 0.1 copy.24
  3.1 0.1 reshape.58
  3.2 0.0 copy-start.3
  3.3 0.0 copy-start.4
  3.3 4.0 %gather_fusion.1 = f32[256]{0:T(256)S(1)} fusion(f32[64,4,16032]{2,1,0:T(4,128)} %param.11, s32[256]{0:T(256)S(1)} %reshape.58), kind=kCustom, calls=%fused_computation.1.clone | custom fusion | bytes 5120 | tf_op jit(solution)/shard_map/jit(take_along_axis)/gather | solution.py:22
  7.3 0.1 reshape.67
  7.4 0.1 copy.27
  7.5 0.0 copy-done.4
  7.5 37.8 %fusion.20 = (f32[64,5]{0,1:T(8,128)S(1)}, f32[64,5,16032]{2,0,1:T(8,128)}) fusion(f32[64]{0:T(128)S(1)} %copy-done.4, bf16[2048,16032]{0,1:T(8,128)(2,1)} %param.10, bf16[64,5,2048]{2,0,1:T(8,128)(2,1)S(1)} %copy-done, f32[2048]{0:T(1024)S(1)} %copy-done.3, f32[64,5]{0,1:T(8,128)S(1)} %add_rsqrt_fusion), kind=kOutput, calls=%fused_computation.37 | convolution fusion | flops 21026344960 | bytes 87509760 | tf_op jit(solution)/shard_map/cle,ew->clw/dot_general | solution.py:14
  45.3 13.8 %pmax.7 = f32[64,5]{0,1:T(8,128)S(1)} all-reduce(f32[64,5]{0,1:T(8,128)S(1)} %get-tuple-element.29), channel_id=1, replica_groups=mesh['dp'=4,'tp'=8] {'tp'}, use_global_device_ids=true, to_apply=%region_3.5 | all-reduce | flops 320 | bytes 2560 | tf_op jit(solution)/shard_map/pmax | solution.py:16
  59.1 9.7 %exponential_reduce_fusion = f32[64,5]{0,1:T(8,128)S(1)} fusion(f32[64,5,16032]{2,0,1:T(8,128)} %get-tuple-element.30, f32[64,5]{0,1:T(8,128)S(1)} %pmax.7), kind=kLoop, calls=%fused_computation.4 | loop fusion | flops 10260160 | bytes 20523520 | tf_op jit(solution)/shard_map/reduce_sum | solution.py:17
  68.9 14.8 %psum.29 = f32[64,5]{0,1:T(8,128)S(1)} all-reduce(f32[64,5]{0,1:T(8,128)S(1)} %exponential_reduce_fusion), channel_id=1, replica_groups=mesh['dp'=4,'tp'=8] {'tp'}, use_global_device_ids=true, to_apply=%region_5.7 | all-reduce | flops 320 | bytes 2560 | tf_op jit(solution)/shard_map/psum | solution.py:23
  83.7 0.5 slice_bitcast_fusion
  84.2 22.1 %fusion.6 = (f32[64,4]{0,1:T(4,128)S(1)}, f32[64,4,16032]{2,0,1:T(8,128)}) fusion(f32[64,4,16032]{2,1,0:T(4,128)} %param.11, f32[64,4]{0,1:T(4,128)S(1)} %slice.11, f32[64,5,16032]{2,0,1:T(8,128)} %get-tuple-element.30), kind=kLoop, calls=%fused_computation.9 | loop fusion | flops 16416512 | bytes 49252352 | tf_op jit(solution)/shard_map/reduce_sum | solution.py:29
  106.3 4.6 %gather_fusion = f32[256]{0:T(256)S(1)} fusion(f32[64,4,16032]{2,0,1:T(8,128)} %get-tuple-element.28, s32[256]{0:T(256)S(1)} %reshape.58), kind=kCustom, calls=%fused_computation.clone | custom fusion | bytes 5120 | tf_op jit(solution)/shard_map/jit(take_along_axis)/gather | solution.py:21
  110.9 0.1 reshape.61
  111.0 0.1 copy.25
  111.2 12.7 %all-reduce = (f32[64,4]{0,1:T(4,128)S(1)}, f32[64,4]{0,1:T(4,128)S(1)}, f32[64,4]{0,1:T(4,128)S(1)}) all-reduce(f32[64,4]{0,1:T(4,128)S(1)} %bitcast_select_fusion, f32[64,4]{0,1:T(4,128)S(1)} %get-tuple-element.24, f32[64,4]{0,1:T(4,128)S(1)} %get-tuple-element.27), channel_id=1, replica_groups=mesh['dp'=4,'tp'=8] {'tp'}, use_global_device_ids=true, to_apply=%region_6.8 | all-reduce | flops 768 | bytes 6144 | tf_op jit(solution)/shard_map/psum | solution.py:23
  123.8 0.0 copy-start.2
  123.9 12.7 %broadcast_divide_fusion = f32[64,4,16032]{2,0,1:T(8,128)S(1)} fusion(f32[64,4]{0,1:T(4,128)S(1)} %get-tuple-element.23, f32[64,4,16032]{2,1,0:T(4,128)} %param.11, f32[64,4]{0,1:T(4,128)S(1)} %slice.11, f32[64,5,16032]{2,0,1:T(8,128)} %get-tuple-element.30), kind=kLoop, calls=%fused_computation.8 | loop fusion | flops 16416768 | bytes 49252352 | tf_op jit(solution)/shard_map/div | solution.py:30
  136.6 11.8 %copy.29 = f32[64,4,16032]{2,1,0:T(4,128)} copy(f32[64,4,16032]{2,0,1:T(8,128)S(1)} %broadcast_divide_fusion) | data formatting | bytes 32833536
  148.3 0.6 fusion.18
  (15 shorter events, 0.1 us)
Async XLA Ops:
  3.2 4.2 %copy-start = (bf16[64,5,2048]{2,0,1:T(8,128)(2,1)S(1)}, bf16[64,5,2048]{2,0,1:T(8,128)(2,1)}, u32[]{:S(2)}) copy-start(bf16[64,5,2048]{2,0,1:T(8,128)(2,1)} %param.8) | copy-start | bytes 3932164
  3.2 4.2 %copy-start.3 = (f32[2048]{0:T(1024)S(1)}, f32[2048]{0:T(1024)}, u32[]{:S(2)}) copy-start(f32[2048]{0:T(1024)} %param.9) | copy-start | bytes 24580
  3.3 4.2 %copy-start.4 = (f32[64]{0:T(128)S(1)}, f32[64]{0:T(128)}, u32[]{:S(2)}) copy-start(f32[64]{0:T(128)} %param.13) | copy-start | bytes 772
  106.3 4.8 %copy-start.1 = (s32[64,4]{0,1:T(4,128)S(1)}, s32[64,4]{0,1:T(4,128)}, u32[]{:S(2)}) copy-start(s32[64,4]{0,1:T(4,128)} %param.12) | copy-start | bytes 3076
  123.8 12.7 %copy-start.2 = (f32[64,4]{0,1:T(4,128)}, f32[64,4]{0,1:T(4,128)S(1)}, u32[]{:S(2)}) copy-start(f32[64,4]{0,1:T(4,128)S(1)} %get-tuple-element.23) | copy-start | bytes 3076
where the time goes:
time: 149 us
  other arithmetic  47.5 us (32%)
  blocking collectives  41.3 us (28%)
  matrix products  37.8 us (25%)
  local copies, waits for them, and re-layouts  21.5 us (14%)
    dot_general x1, matrix products, local_step(): jnp.einsum('cle,ew->clw', normed, w_head, preferred_element_type=jnp.floa...  37.8 us
    psum x2, blocking collectives, local_step(): lax.psum((local_sum, tok_scaled, tok_draft), 'tp')  27.5 us
    reduce_sum x1, other arithmetic, local_step(): norm_sum = lax.psum(jnp.sum(excess, axis=-1), 'tp')  22.1 us
    pmax x1, blocking collectives, local_step(): row_max = lax.pmax(jnp.max(scaled, axis=-1), 'tp')  13.8 us
    div x1, other arithmetic, local_step(): residual = excess / norm_sum[:, :, None]  12.7 us
    unnamed x11, local copies, waits for them, and re-layouts  11.8 us
    reduce_sum x1, other arithmetic, local_step(): local_sum = jnp.sum(jnp.exp(scaled - row_max[:, :, None]), axis=-1)  9.73 us
    gather x5, local copies, waits for them, and re-layouts, local_step(): jnp.take_along_axis(scaled[:, :draft_len], safe_idx, axis=-1)[:, :, 0]  5 us

commit v1 on v0

v1 whole, which is shorter than its diff:
```python
import functools

import jax
import jax.numpy as jnp
from jax import lax
from jax.experimental import pallas as pl
from jax.experimental.pallas import tpu as pltpu
from jax.sharding import PartitionSpec as P

LANES = 128
TILE = 256
STEP = 2 * TILE
RING = 8
GRANT = 24 * 1024 * 1024
LOG2E = 1.4426950408889634
LN2 = 0.6931471805599453
LOWEST = -3.4028234e38
MESH = pl.DeviceIdType.MESH


def _row_to_col(row):
    n = row.shape[1]
    r = lax.broadcasted_iota(jnp.int32, (n, n), 0)
    c = lax.broadcasted_iota(jnp.int32, (n, n), 1)
    return jnp.sum(jnp.where(r == c, row, 0.0), axis=1, keepdims=True)


def _col_to_row(col):
    n = col.shape[0]
    r = lax.broadcasted_iota(jnp.int32, (n, n), 0)
    c = lax.broadcasted_iota(jnp.int32, (n, n), 1)
    return jnp.sum(jnp.where(r == c, col, 0.0), axis=0, keepdims=True)


def _logits_kernel(
    dims,
    x_hbm, gain_ref, w_hbm, q_hbm, temp_ref,
    s_ref, q_buf, msg1,
    h_buf, x_buf, w_buf, q_last, m_buf, l_buf, scale_buf,
    h_sem, w_sem, q_sem,
):
    batch, draft, depth, vocab = dims
    rows = batch * (draft + 1)
    nk = depth // TILE
    full = vocab // STEP
    rest = vocab - full * STEP
    nc = -(-vocab // LANES)
    last = vocab - (nc - 1) * LANES
    def w_copy(n, size=STEP):
        slot = lax.rem(n, RING)
        return pltpu.make_async_copy(
            w_hbm.at[pl.ds(n * STEP, size), :], w_buf.at[slot, pl.ds(0, size), :], w_sem.at[slot])

    qv = q_buf.reshape(nc, batch, draft, LANES)

    def q_copy(c):
        return pltpu.make_async_copy(
            q_hbm.at[:, :, pl.ds(pl.multiple_of(c * LANES, LANES), LANES)], qv.at[c], q_sem.at[c])

    def last_q():
        return pltpu.make_async_copy(
            q_hbm.at[:, :, pl.ds((nc - 1) * LANES, last)], q_last, q_sem.at[nc - 1])

    h_copy = pltpu.make_async_copy(x_hbm, h_buf, h_sem)
    h_copy.start()
    for n in range(RING - 1):
        w_copy(n).start()

    temp_col = _row_to_col(temp_ref[...])
    scale_buf[...] = jnp.broadcast_to(LOG2E / temp_col, (batch, LANES))
    m_buf[...] = jnp.full_like(m_buf, LOWEST)
    l_buf[...] = jnp.zeros_like(l_buf)

    h_copy.wait()

    @pl.loop(0, rows // 16)
    def _(i):
        sl = pl.ds(pl.multiple_of(i * 16, 16), 16)
        h = h_buf[sl, :].astype(jnp.float32)
        r = lax.rsqrt(jnp.mean(h * h, axis=-1, keepdims=True) + 1e-5)
        x_buf[sl, :] = (h * r * gain_ref[...]).astype(jnp.bfloat16)

    groups = draft + 1

    def online(g, q, c0, z, ncol, penalty=None):
        rs = pl.ds(g * batch, batch)
        scale = scale_buf[...]
        ss = [z[:, i * LANES:(i + 1) * LANES] * scale for i in range(ncol)]
        if penalty is not None:
            ss = [s + p for s, p in zip(ss, penalty)]
        m_old = m_buf[rs, :]
        m_new = m_old
        for s in ss:
            m_new = jnp.maximum(m_new, s)
        l = l_buf[rs, :] * jnp.exp2(m_old - m_new)
        for s in ss:
            l = l + jnp.exp2(s - m_new)
        m_buf[rs, :] = m_new
        l_buf[rs, :] = l
        if g < draft:
            for i in range(ncol):
                s_ref[c0 + i, pl.ds(g, batch, stride=draft), :] = ss[i]

    def lhs(g, k):
        return x_buf[pl.ds(g * batch, batch), pl.ds(k * TILE, TILE)]

    def push(n, q, k):
        slot = lax.rem(n, RING)
        w = w_buf[slot, pl.ds(q * TILE, TILE), pl.ds(k * TILE, TILE)]
        pltpu.matmul_push_rhs(w, staging_register=k % 2, mxu_index=q, transpose=True)

    def mxu_body(*accs):
        acc = [[[accs[(a * 2 + q) * groups + g] for g in range(groups)] for q in range(2)] for a in range(2)]
        for a in range(2):
            for q in range(2):
                for g in range(groups):
                    pltpu.matmul_pop(acc[a][q][g])

        def fullstep(n, a, issue, penalty=None, next_full=True):
            old = acc[1 - a]
            c_old = jnp.maximum(n - 1, 0) * (STEP // LANES)
            for k in range(nk):
                for q in range(2):
                    for g in range(groups):
                        pltpu.matmul_acc_lhs(acc[a][q][g], lhs(g, k), load_staged_rhs=k % 2 if g == 0 else None)
                for q in range(2):
                    if k + 1 < nk:
                        push(n, q, k + 1)
                    elif next_full:
                        push(n + 1, q, 0)
                if k == 1:
                    issue()
                if 1 <= k <= groups:
                    g = k - 1
                    for q in range(2):
                        z = pltpu.matmul_pop(old[q][g])
                        online(g, q, c_old + q * (TILE // LANES), z, TILE // LANES,
                               None if penalty is None else [penalty] * (TILE // LANES))

        w_copy(0).wait()
        for q in range(2):
            push(0, q, 0)

        split = (full - (RING - 1)) // 2 * 2
        tail = full // 2 * 2
        early = 2
        per = 8
        mid = nc - 1 - early * split - per * (tail - split)

        def issue_early(n):
            w_copy(n + RING - 1).start()
            for i in range(early):
                q_copy(n * early + i).start()

        def issue_late(n):
            for i in range(per):
                q_copy(early * split + mid + (n - split) * per + i).start()

        @pl.loop(0, split // 2)
        def _(i):
            n = 2 * i
            w_copy(n + 1).wait()
            fullstep(n, 0, lambda: issue_early(n), penalty=jnp.where(i == 0, LOWEST, 0.0).astype(jnp.float32))
            w_copy(n + 2).wait()
            fullstep(n + 1, 1, lambda: issue_early(n + 1))

        w_copy(full, rest).start()

        last_q().start()

        @pl.loop(0, mid)
        def _(i):
            q_copy(early * split + i).start()

        @pl.loop(split // 2, tail // 2)
        def _(i):
            n = 2 * i
            w_copy(n + 1).wait()
            fullstep(n, 0, lambda: issue_late(n))
            w_copy(n + 2).wait()
            fullstep(n + 1, 1, lambda: issue_late(n + 1))

        assert tail == full - 1
        n = full - 1
        w_copy(full, rest).wait()
        fullstep(n, 0, lambda: None, next_full=False)
        slot = full % RING
        half = nk // 2
        for kk in range(half):
            for q in range(2):
                k = q * half + kk
                w = w_buf[slot, pl.ds(0, TILE), pl.ds(k * TILE, TILE)]
                pltpu.matmul_push_rhs(w, staging_register=kk % 2, mxu_index=q, transpose=True)
                for g in range(groups):
                    pltpu.matmul_acc_lhs(acc[1][q][g], lhs(g, k), load_staged_rhs=kk % 2 if g == 0 else None)
        for g in range(groups):
            for q in range(2):
                z = pltpu.matmul_pop(acc[0][q][g])
                online(g, q, n * (STEP // LANES) + q * (TILE // LANES), z, TILE // LANES)
        ncol = -(-rest // LANES)
        lane = lax.broadcasted_iota(jnp.int32, (batch, LANES), 1)
        pens = [None] * ncol
        for i in range(ncol):
            pens[i] = jnp.where(lane + i * LANES < rest, 0.0, LOWEST)
        for g in range(groups):
            z = pltpu.matmul_pop(acc[1][0][g]) + pltpu.matmul_pop(acc[1][1][g])
            online(g, 0, full * (STEP // LANES), z, ncol, pens)

    specs = [pltpu.ACC(q)((batch, TILE), jnp.float32) for a in range(2) for q in range(2) for g in range(groups)]
    pl.run_scoped(mxu_body, *specs)

    msg1[...] = jnp.zeros_like(msg1)
    for g in range(groups):
        rs = pl.ds(g * batch, batch)
        m = m_buf[rs, :]
        top = jnp.max(m, axis=1, keepdims=True)
        tot = jnp.sum(l_buf[rs, :] * jnp.exp2(m - top), axis=1, keepdims=True)
        msg1[pl.ds(g, 1), pl.ds(0, batch)] = _col_to_row(top + jnp.log2(tot))

    @pl.loop(0, nc - 1)
    def _(c):
        q_copy(c).wait()

    last_q().wait()
    for b in range(0, batch, 2):
        q_buf[nc - 1, pl.ds(b * draft, 2 * draft), pl.ds(0, last)] = jnp.concatenate([q_last[b], q_last[b + 1]], axis=0)


def _verify_kernel(
    dims,
    s_ref, q_ref, msg1, tok_smem, tok_ref,
    col_buf, inv_ref, accept_ref, norm_ref, bonus_ref,
    gs_buf, gq_buf, part_buf,
    msg2, got1, got2,
    send1, recv1, send2, recv2,
):
    batch, draft, vocab, ntp = dims
    nc = -(-vocab // LANES)
    last = vocab - (nc - 1) * LANES
    me = lax.axis_index("tp")
    barrier = pltpu.get_barrier_semaphore()
    for d in range(1, ntp):
        pl.semaphore_signal(barrier, inc=1, device_id={"tp": lax.rem(me + d, ntp)}, device_id_type=MESH)
    pl.semaphore_wait(barrier, ntp - 1)

    def remote(msg, got, send, recv, d):
        return pltpu.make_async_remote_copy(
            src_ref=msg, dst_ref=got.at[me], send_sem=send.at[d], recv_sem=recv.at[me],
            device_id={"tp": lax.rem(me + d, ntp)}, device_id_type=MESH)

    def arrived(msg, got, send, recv, d):
        src = lax.rem(me + d, ntp)
        return pltpu.make_async_remote_copy(
            src_ref=msg, dst_ref=got.at[src], send_sem=send.at[d], recv_sem=recv.at[src],
            device_id={"tp": src}, device_id_type=MESH)

    for d in range(1, ntp):
        remote(msg1, got1, send1, recv1, d).start()
    got1[me] = msg1[...]

    @pl.loop(0, batch)
    def _(b):
        for j in range(draft):
            idx = tok_smem[j, b] - me * vocab
            idx = jnp.minimum(jnp.maximum(idx, 0), vocab - 1)
            c = lax.shift_right_logical(idx, 7)
            gs_buf[pl.ds(j * batch + b, 1), :] = s_ref[c, pl.ds(b * draft + j, 1), :]
            gq_buf[pl.ds(j * batch + b, 1), :] = q_ref[c, pl.ds(b * draft + j, 1), :]

    msg2[...] = jnp.zeros_like(msg2)
    lane = lax.broadcasted_iota(jnp.int32, (batch, LANES), 1)
    for j in range(draft):
        idx = _row_to_col(tok_ref[pl.ds(j, 1), :].astype(jnp.float32)).astype(jnp.int32) - me * vocab
        owned = jnp.logical_and(idx >= 0, idx < vocab)
        hit = jnp.logical_and(owned, lane == jnp.bitwise_and(idx, LANES - 1))
        rs = pl.ds(j * batch, batch)
        tok_s = jnp.sum(jnp.where(hit, gs_buf[rs, :], 0.0), axis=1, keepdims=True)
        tok_q = jnp.sum(jnp.where(hit, gq_buf[rs, :], 0.0), axis=1, keepdims=True)
        msg2[pl.ds(draft + j, 1), pl.ds(0, batch)] = _col_to_row(tok_s)
        msg2[pl.ds(2 * draft + j, 1), pl.ds(0, batch)] = _col_to_row(tok_q)

    for d in range(1, ntp):
        arrived(msg1, got1, send1, recv1, d).wait_recv()
    top = got1[0]
    for i in range(1, ntp):
        top = jnp.maximum(top, got1[i])
    tot = jnp.exp2(got1[0] - top)
    for i in range(1, ntp):
        tot = tot + jnp.exp2(got1[i] - top)
    lse2 = top + jnp.log2(tot)
    bonus_ref[...] = lse2[draft:draft + 1, 0:batch] * LN2
    for j in range(draft):
        col_buf[pl.ds(j, batch, stride=draft), :] = jnp.broadcast_to(
            _row_to_col(lse2[j:j + 1, 0:batch]), (batch, LANES))

    nv = batch * draft // 8
    unroll = 25 if (nc - 1) % 25 == 0 else 1
    last_mask = lax.broadcasted_iota(jnp.int32, (8, LANES), 1) < last

    @pl.loop(0, nv // 2)
    def _(v):
        rss = [pl.ds(pl.multiple_of((2 * v + i) * 8, 8), 8) for i in range(2)]
        ls = [col_buf[rs, :] for rs in rss]

        def ex(c, i):
            return jnp.maximum(jnp.exp2(s_ref[c, rss[i], :] - ls[i]) - q_ref[c, rss[i], :], 0.0)

        def inner(t, sums):
            sums = list(sums)
            for u in range(unroll):
                c = t * unroll + u
                for i in range(2):
                    sums[i] = sums[i] + ex(c, i)
            return tuple(sums)

        zero = jnp.zeros((8, LANES), jnp.float32)
        sums = lax.fori_loop(0, (nc - 1) // unroll, inner, (zero, zero))
        for i in range(2):
            e = jnp.where(last_mask, ex(nc - 1, i), 0.0)
            part_buf[rss[i], :] = sums[i] + e

    for j in range(draft):
        part = jnp.sum(part_buf[pl.ds(j, batch, stride=draft), :], axis=1, keepdims=True)
        msg2[pl.ds(j, 1), pl.ds(0, batch)] = _col_to_row(part)

    for d in range(1, ntp):
        remote(msg2, got2, send2, recv2, d).start()
    got2[me] = msg2[...]
    for d in range(1, ntp):
        arrived(msg2, got2, send2, recv2, d).wait_recv()
    tot = got2[0]
    for i in range(1, ntp):
        tot = tot + got2[i]
    norm = tot[0:draft, 0:batch]
    norm_ref[...] = norm
    target = jnp.exp2(tot[draft:2 * draft, 0:batch] - lse2[0:draft, 0:batch])
    accept_ref[...] = jnp.minimum(1.0, target / tot[2 * draft:3 * draft, 0:batch])
    for j in range(draft):
        inv_ref[pl.ds(j, batch, stride=draft), :] = jnp.broadcast_to(
            1.0 / _row_to_col(norm[j:j + 1, :]), (batch, LANES))
    for d in range(1, ntp):
        remote(msg1, got1, send1, recv1, d).wait_send()
        remote(msg2, got2, send2, recv2, d).wait_send()


OUT_RING = 4
OUT_GROUP = 5


def _write_kernel(
    dims, s_ref, q_ref, lse_ref, inv_ref, accept_in, norm_in, bonus_in,
    out_hbm, accept_ref, norm_ref, bonus_ref, stage, stage_last, sem,
):
    batch, draft, vocab = dims
    accept_ref[...] = accept_in[...]
    norm_ref[...] = norm_in[...]
    bonus_ref[...] = bonus_in[...]
    nc = -(-vocab // LANES)
    view = stage.reshape(OUT_RING * OUT_GROUP, batch, draft, LANES)
    ngroups = (nc - 1) // OUT_GROUP
    assert ngroups * OUT_GROUP == nc - 1

    def copy(slot, c):
        return pltpu.make_async_copy(
            view.at[slot], out_hbm.at[:, :, pl.ds(pl.multiple_of(c * LANES, LANES), LANES)], sem.at[slot])

    def fill(slot, c):
        stage[slot] = jnp.maximum(jnp.exp2(s_ref[c] - lse_ref[...]) - q_ref[c], 0.0) * inv_ref[...]

    @pl.loop(0, ngroups)
    def _(t):
        base = lax.rem(t, OUT_RING) * OUT_GROUP

        @pl.when(t >= OUT_RING)
        def _():
            for i in range(OUT_GROUP):
                copy(base + i, (t - OUT_RING) * OUT_GROUP + i).wait()

        for i in range(OUT_GROUP):
            fill(base + i, t * OUT_GROUP + i)
            copy(base + i, t * OUT_GROUP + i).start()

    for t in range(ngroups - OUT_RING, ngroups):
        for i in range(OUT_GROUP):
            copy(t % OUT_RING * OUT_GROUP + i, t * OUT_GROUP + i).wait()
    c = nc - 1
    last = vocab - c * LANES
    fill(0, c)
    for b in range(batch):
        rs = pl.ds(b * draft, draft)
        stage_last[b] = stage[0, rs, pl.ds(0, last)]
    final = pltpu.make_async_copy(stage_last, out_hbm.at[:, :, pl.ds(c * LANES, last)], sem.at[0])
    final.start()
    final.wait()


def solution(mesh):
    ntp = mesh.shape["tp"]

    def local_step(hidden, norm_gain, w_head, draft_probs, draft_tokens, temperature):
        batch, draft, vocab = draft_probs.shape
        depth = hidden.shape[2]
        rows = batch * (draft + 1)
        nc = -(-vocab // LANES)
        vmem = pl.BlockSpec(memory_space=pltpu.VMEM)
        hbm = pl.BlockSpec(memory_space=pl.ANY)
        smem = pl.BlockSpec(memory_space=pltpu.SMEM)
        keep = functools.partial(pltpu.with_memory_space_constraint, memory_space=pltpu.VMEM)
        f32, bf16, dma = jnp.float32, jnp.bfloat16, pltpu.SemaphoreType.DMA
        vec = pltpu.VMEM((batch * draft, LANES), f32)
        big = pltpu.VMEM((nc, batch * draft, LANES), f32)
        x = hidden.transpose(1, 0, 2).reshape(rows, depth)
        tok = draft_tokens.T
        s, q, lse = pl.pallas_call(
            functools.partial(_logits_kernel, (batch, draft, depth, vocab)),
            out_shape=(big, big, pltpu.VMEM((8, LANES), f32)),
            in_specs=[hbm, vmem, hbm, hbm, vmem],
            out_specs=(vmem,) * 3,
            scratch_shapes=[
                pltpu.VMEM((rows, depth), bf16),
                pltpu.VMEM((rows, depth), bf16),
                pltpu.VMEM((RING, STEP, depth), bf16),
                pltpu.VMEM((batch, draft, vocab - (nc - 1) * LANES), f32),
                pltpu.VMEM((rows, LANES), f32),
                pltpu.VMEM((rows, LANES), f32),
                pltpu.VMEM((batch, LANES), f32),
                dma,
                dma((RING,)),
                dma((nc,)),
            ],
            compiler_params=pltpu.CompilerParams(vmem_limit_bytes=GRANT),
            name="logits",
        )(x, norm_gain.reshape(1, depth), w_head.T, draft_probs, temperature.reshape(1, batch))
        lse, inv, accept, norm, bonus = pl.pallas_call(
            functools.partial(_verify_kernel, (batch, draft, vocab, ntp)),
            out_shape=(
                vec,
                vec,
                pltpu.VMEM((draft, batch), f32),
                pltpu.VMEM((draft, batch), f32),
                pltpu.VMEM((1, batch), f32),
            ),
            in_specs=[vmem, vmem, vmem, smem, vmem],
            out_specs=(vmem,) * 5,
            scratch_shapes=[
                vec, vec, vec,
                pltpu.VMEM((16, LANES), f32),
                pltpu.VMEM((ntp, 8, LANES), f32),
                pltpu.VMEM((ntp, 16, LANES), f32),
                dma((ntp,)), dma((ntp,)), dma((ntp,)), dma((ntp,)),
            ],
            compiler_params=pltpu.CompilerParams(
                collective_id=0, has_side_effects=True, vmem_limit_bytes=GRANT),
            name="verify",
        )(keep(s), keep(q), keep(lse), tok, tok)
        residual, accept, norm, bonus = pl.pallas_call(
            functools.partial(_write_kernel, (batch, draft, vocab)),
            out_shape=(
                jax.ShapeDtypeStruct(draft_probs.shape, f32),
                jax.ShapeDtypeStruct((draft, batch), f32),
                jax.ShapeDtypeStruct((draft, batch), f32),
                jax.ShapeDtypeStruct((1, batch), f32),
            ),
            in_specs=[vmem] * 7,
            out_specs=(hbm, vmem, vmem, vmem),
            scratch_shapes=[
                pltpu.VMEM((OUT_RING * OUT_GROUP, batch * draft, LANES), f32),
                pltpu.VMEM((batch, draft, vocab - (nc - 1) * LANES), f32),
                dma((OUT_RING * OUT_GROUP,)),
            ],
            compiler_params=pltpu.CompilerParams(vmem_limit_bytes=GRANT),
            name="write",
        )(*map(keep, (s, q, lse, inv, accept, norm, bonus)))
        return accept.T, norm.T, residual, bonus.reshape(batch)

    return jax.shard_map(
        local_step,
        mesh=mesh,
        in_specs=(P('dp', None, None), P(), P(None, 'tp'), P('dp', None, 'tp'), P('dp', None), P('dp')),
        out_specs=(P('dp', None), P('dp', None), P('dp', None, 'tp'), P('dp')),
        check_vma=False,
    )
```

time: 149 us -> 58.9 us (0.40)
  Pallas kernels: 0 us -> 58.1 us
  other arithmetic: 47.5 us -> 0 us
  blocking collectives: 41.3 us -> 0 us
  matrix products: 37.8 us -> 0 us
  local copies, waits for them, and re-layouts: 21.5 us -> 0 us
    pallas_call x0 -> x3, Pallas kernels: none -> 58.1 us  [the longest x1 34.1 us: local_step(): pl.pallas_call(functools.partial(_logits_kernel, (batch, draft, depth, vo...]
    dot_general x1 -> x0, matrix products: 37.8 us -> none  [local_step(): jnp.einsum('cle,ew->clw', normed, w_head, preferred_element_type=jnp.floa...]
    reduce_sum x3 -> x0, other arithmetic: 33.5 us -> none  [the longest x1 22.1 us: local_step(): norm_sum = lax.psum(jnp.sum(excess, axis=-1), 'tp')]
    psum x2 -> x0, blocking collectives: 27.5 us -> none  [local_step(): lax.psum((local_sum, tok_scaled, tok_draft), 'tp')]
    pmax x1 -> x0, blocking collectives: 13.8 us -> none  [local_step(): row_max = lax.pmax(jnp.max(scaled, axis=-1), 'tp')]
    div x1 -> x0, other arithmetic: 12.7 us -> none  [local_step(): residual = excess / norm_sum[:, :, None]]
    unnamed x11 -> x0, local copies, waits for them, and re-layouts: 11.8 us -> none
    gather x8 -> x0, local copies, waits for them, and re-layouts: 9.19 us -> none  [the longest x5 5 us: local_step(): jnp.take_along_axis(scaled[:, :draft_len], safe_idx, axis=-1)[:, :, 0]]
where the time goes in v1:
time: 58.9 us; the launch traced here: 58.8 us
  Pallas kernels  58.1 us (99%)
  between operations  0.65 us (1%)
    pallas_call x1, Pallas kernels, local_step(): pl.pallas_call(functools.partial(_logits_kernel, (batch, draft, depth, vo...  34.1 us
    pallas_call x1, Pallas kernels, local_step(): pl.pallas_call(functools.partial(_verify_kernel, (batch, draft, vocab, nt...  16.6 us
    pallas_call x1, Pallas kernels, local_step(): pl.pallas_call(functools.partial(_write_kernel, (batch, draft, vocab)), o...  7.47 us

profile of v1, /device:TPU:81, one launch (start us, length us, event | category | flops | bytes accessed | tf_op | source)
XLA Modules:
  0.0 58.8 jit_solution(15904516201419211451)
XLA Ops:
  0.6 34.1 %logits.1 = (f32[126,256,128]{2,1,0:T(8,128)S(1)}, f32[126,256,128]{2,1,0:T(8,128)S(1)}, f32[8,128]{1,0:T(8,128)S(1)}) custom-call(bf16[320,2048]{1,0:T(8,128)(2,1)} %bitcast.11, f32[1,2048]{1,0:T(1,128)} %bitcast.12, bf16[16032,2048]{1,0:T(8,128)(2,1)} %bitcast.10, f32[64,4,16032]{2,1,0:T(4,128)} %q_hbm.1, f32[1,64]{1,0:T(1,128)} %bitcast.15), custom_call_target="tpu_custom_call" | custom-call | tf_op jit(solution)/shard_map/logits/pallas_call | solution.py:414
  34.7 16.6 %verify.1 = (f32[256,128]{1,0:T(8,128)S(1)}, f32[256,128]{1,0:T(8,128)S(1)}, f32[4,64]{1,0:T(4,128)S(1)}, f32[4,64]{1,0:T(4,128)S(1)}, f32[1,64]{1,0:T(1,128)S(1)}) custom-call(f32[126,256,128]{2,1,0:T(8,128)S(1)} %get-tuple-element.16.s_ref, f32[126,256,128]{2,1,0:T(8,128)S(1)} %get-tuple-element.17.q_ref, f32[8,128]{1,0:T(8,128)S(1)} %get-tuple-element.18.msg1, ...), custom_call_target="tpu_custom_call" | custom-call | tf_op jit(solution)/shard_map/verify/pallas_call | solution.py:434
  51.3 7.5 %write.1 = (f32[64,4,16032]{2,1,0:T(4,128)}, f32[4,64]{1,0:T(4,128)}, f32[4,64]{1,0:T(4,128)}, f32[1,64]{1,0:T(1,128)}) custom-call(f32[126,256,128]{2,1,0:T(8,128)S(1)} %get-tuple-element.16.s_ref, f32[126,256,128]{2,1,0:T(8,128)S(1)} %get-tuple-element.17.q_ref, f32[256,128]{1,0:T(8,128)S(1)} %get-tuple-element.19.lse_ref, ...), custom_call_target="tpu_custom_call" | custom-call | tf_op jit(solution)/shard_map/write/pallas_call | solution.py:456

commit v2 on v1

--- a/solution.py
+++ b/solution.py
@@ -11,6 +11,10 @@
 TILE = 256
 STEP = 2 * TILE
 RING = 8
+W_PARTS = 4
+FENCES = 6
+SIG = (1, 3, 5, 7)
+GRP = {1: (0,), 3: (1, 2), 5: (3, 4)}
 GRANT = 24 * 1024 * 1024
 LOG2E = 1.4426950408889634
 LN2 = 0.6931471805599453
@@ -35,9 +39,9 @@
 def _logits_kernel(
     dims,
     x_hbm, gain_ref, w_hbm, q_hbm, temp_ref,
-    s_ref, q_buf, msg1,
-    h_buf, x_buf, w_buf, q_last, m_buf, l_buf, scale_buf,
-    h_sem, w_sem, q_sem,
+    s_ref, q_buf, m_buf, l_buf,
+    h_buf, x_buf, w_buf, q_last, scale_buf,
+    h_sem, w_sem, q_sem, fence,
 ):
     batch, draft, depth, vocab = dims
     rows = batch * (draft + 1)
@@ -46,39 +50,41 @@
     rest = vocab - full * STEP
     nc = -(-vocab // LANES)
     last = vocab - (nc - 1) * LANES
-    def w_copy(n, size=STEP):
+    part = STEP // W_PARTS
+
+    def w_copy(n, i, size=part):
         slot = lax.rem(n, RING)
         return pltpu.make_async_copy(
-            w_hbm.at[pl.ds(n * STEP, size), :], w_buf.at[slot, pl.ds(0, size), :], w_sem.at[slot])
+            w_hbm.at[pl.ds(n * STEP + i * part, size), :], w_buf.at[slot, pl.ds(i * part, size), :], w_sem.at[slot, i])
+
+    def w_wait(n):
+        for i in range(W_PARTS):
+            w_copy(n, i).wait()
+
+    def w_rest():
+        return [w_copy(full, i, min(part, rest - i * part)) for i in range(-(-rest // part))]
 
     qv = q_buf.reshape(nc, batch, draft, LANES)
 
     def q_copy(c):
         return pltpu.make_async_copy(
-            q_hbm.at[:, :, pl.ds(pl.multiple_of(c * LANES, LANES), LANES)], qv.at[c], q_sem.at[c])
+            q_hbm.at[:, :, pl.ds(pl.multiple_of(c * LANES, LANES), LANES)], qv.at[c], q_sem.at[0])
 
     def last_q():
         return pltpu.make_async_copy(
-            q_hbm.at[:, :, pl.ds((nc - 1) * LANES, last)], q_last, q_sem.at[nc - 1])
+            q_hbm.at[:, :, pl.ds((nc - 1) * LANES, last)], q_last, q_sem.at[1])
 
     h_copy = pltpu.make_async_copy(x_hbm, h_buf, h_sem)
     h_copy.start()
     for n in range(RING - 1):
-        w_copy(n).start()
+        for i in range(W_PARTS):
+            w_copy(n, i).start()
+    last_q().start(priority=1)
 
     temp_col = _row_to_col(temp_ref[...])
     scale_buf[...] = jnp.broadcast_to(LOG2E / temp_col, (batch, LANES))
     m_buf[...] = jnp.full_like(m_buf, LOWEST)
     l_buf[...] = jnp.zeros_like(l_buf)
-
-    h_copy.wait()
-
-    @pl.loop(0, rows // 16)
-    def _(i):
-        sl = pl.ds(pl.multiple_of(i * 16, 16), 16)
-        h = h_buf[sl, :].astype(jnp.float32)
-        r = lax.rsqrt(jnp.mean(h * h, axis=-1, keepdims=True) + 1e-5)
-        x_buf[sl, :] = (h * r * gain_ref[...]).astype(jnp.bfloat16)
 
     groups = draft + 1
 
@@ -116,6 +122,19 @@
                 for g in range(groups):
                     pltpu.matmul_pop(acc[a][q][g])
 
+        h_copy.wait()
+        for i in range(rows // 32):
+            sl = pl.ds(i * 32, 32)
+            h = h_buf[sl, :].astype(jnp.float32)
+            r = lax.rsqrt(jnp.mean(h * h, axis=-1, keepdims=True) + 1e-5)
+            x_buf[sl, :] = (h_buf[sl, :].astype(jnp.float32) * r * gain_ref[...]).astype(jnp.bfloat16)
+
+        half = nk // 2
+
+        def push_rest(q, kk):
+            w = w_buf[full % RING, pl.ds(0, TILE), pl.ds((q * half + kk) * TILE, TILE)]
+            pltpu.matmul_push_rhs(w, staging_register=kk % 2, mxu_index=q, transpose=True)
+
         def fullstep(n, a, issue, penalty=None, next_full=True):
             old = acc[1 - a]
             c_old = jnp.maximum(n - 1, 0) * (STEP // LANES)
@@ -128,71 +147,83 @@
                         push(n, q, k + 1)
                     elif next_full:
                         push(n + 1, q, 0)
-                if k == 1:
-                    issue()
-                if 1 <= k <= groups:
-                    g = k - 1
+                    else:
+                        push_rest(q, 0)
+                if 1 <= k <= FENCES:
+                    issue(k - 1)
+                if k in SIG:
+                    pl.semaphore_signal(fence, 1)
+                for g in GRP.get(k, ()):
                     for q in range(2):
                         z = pltpu.matmul_pop(old[q][g])
                         online(g, q, c_old + q * (TILE // LANES), z, TILE // LANES,
                                None if penalty is None else [penalty] * (TILE // LANES))
 
-        w_copy(0).wait()
+            pl.semaphore_wait(fence, len(SIG))
+
+        w_wait(0)
         for q in range(2):
             push(0, q, 0)
 
         split = (full - (RING - 1)) // 2 * 2
         tail = full // 2 * 2
-        early = 2
-        per = 8
-        mid = nc - 1 - early * split - per * (tail - split)
-
-        def issue_early(n):
-            w_copy(n + RING - 1).start()
-            for i in range(early):
-                q_copy(n * early + i).start()
-
-        def issue_late(n):
-            for i in range(per):
-                q_copy(early * split + mid + (n - split) * per + i).start()
+        early = FENCES - W_PARTS
+        late = 8
+        final = FENCES
+        mid = nc - 1 - early * split - late * (tail - split) - final
+        assert mid >= 0 and tail == full - 1
+
+        def issue_early(n, i):
+            if i < W_PARTS:
+                w_copy(n + RING - 1, i).start()
+            else:
+                q_copy(n * early + i - W_PARTS).start(priority=1)
+
+        def issue_late(n, i):
+            base = early * split + mid + (n - split) * late
+            q_copy(base + i).start(priority=1)
+            if i < late - FENCES:
+                q_copy(base + FENCES + i).start(priority=1)
+
+        def issue_final(i):
+            q_copy(nc - 1 - final + i).start(priority=1)
 
         @pl.loop(0, split // 2)
-        def _(i):
-            n = 2 * i
-            w_copy(n + 1).wait()
-            fullstep(n, 0, lambda: issue_early(n), penalty=jnp.where(i == 0, LOWEST, 0.0).astype(jnp.float32))
-            w_copy(n + 2).wait()
-            fullstep(n + 1, 1, lambda: issue_early(n + 1))
-
-        w_copy(full, rest).start()
-
-        last_q().start()
+        def _(t):
+            n = 2 * t
+            w_wait(n + 1)
+            fullstep(n, 0, lambda i: issue_early(n, i), penalty=jnp.where(t == 0, LOWEST, 0.0).astype(jnp.float32))
+            w_wait(n + 2)
+            fullstep(n + 1, 1, lambda i: issue_early(n + 1, i))
+
+        for copy in w_rest():
+            copy.start()
 
         @pl.loop(0, mid)
         def _(i):
-            q_copy(early * split + i).start()
+            q_copy(early * split + i).start(priority=1)
 
         @pl.loop(split // 2, tail // 2)
-        def _(i):
-            n = 2 * i
-            w_copy(n + 1).wait()
-            fullstep(n, 0, lambda: issue_late(n))
-            w_copy(n + 2).wait()
-            fullstep(n + 1, 1, lambda: issue_late(n + 1))
-
-        assert tail == full - 1
+        def _(t):
+            n = 2 * t
+            w_wait(n + 1)
+            fullstep(n, 0, lambda i: issue_late(n, i))
+            w_wait(n + 2)
+            fullstep(n + 1, 1, lambda i: issue_late(n + 1, i))
+
         n = full - 1
-        w_copy(full, rest).wait()
-        fullstep(n, 0, lambda: None, next_full=False)
-        slot = full % RING
-        half = nk // 2
+        for copy in w_rest():
+            copy.wait()
+        last_q().wait()
+        for b in range(0, batch, 2):
+            q_buf[nc - 1, pl.ds(b * draft, 2 * draft), pl.ds(0, last)] = jnp.concatenate([q_last[b], q_last[b + 1]], axis=0)
+        fullstep(n, 0, issue_final, next_full=False)
         for kk in range(half):
             for q in range(2):
-                k = q * half + kk
-                w = w_buf[slot, pl.ds(0, TILE), pl.ds(k * TILE, TILE)]
-                pltpu.matmul_push_rhs(w, staging_register=kk % 2, mxu_index=q, transpose=True)
                 for g in range(groups):
-                    pltpu.matmul_acc_lhs(acc[1][q][g], lhs(g, k), load_staged_rhs=kk % 2 if g == 0 else None)
+                    pltpu.matmul_acc_lhs(acc[1][q][g], lhs(g, q * half + kk), load_staged_rhs=kk % 2 if g == 0 else None)
+                if kk + 1 < half:
+                    push_rest(q, kk + 1)
         for g in range(groups):
             for q in range(2):
                 z = pltpu.matmul_pop(acc[0][q][g])
@@ -209,29 +240,16 @@
     specs = [pltpu.ACC(q)((batch, TILE), jnp.float32) for a in range(2) for q in range(2) for g in range(groups)]
     pl.run_scoped(mxu_body, *specs)
 
-    msg1[...] = jnp.zeros_like(msg1)
-    for g in range(groups):
-        rs = pl.ds(g * batch, batch)
-        m = m_buf[rs, :]
-        top = jnp.max(m, axis=1, keepdims=True)
-        tot = jnp.sum(l_buf[rs, :] * jnp.exp2(m - top), axis=1, keepdims=True)
-        msg1[pl.ds(g, 1), pl.ds(0, batch)] = _col_to_row(top + jnp.log2(tot))
-
-    @pl.loop(0, nc - 1)
-    def _(c):
-        q_copy(c).wait()
-
-    last_q().wait()
-    for b in range(0, batch, 2):
-        q_buf[nc - 1, pl.ds(b * draft, 2 * draft), pl.ds(0, last)] = jnp.concatenate([q_last[b], q_last[b + 1]], axis=0)
+    bulk = q_buf.at[pl.ds(0, nc - 1)]
+    pltpu.make_async_copy(bulk, bulk, q_sem.at[0]).wait()
 
 
 def _verify_kernel(
     dims,
-    s_ref, q_ref, msg1, tok_smem, tok_ref,
+    s_ref, q_ref, m_ref, l_ref, tok_smem, tok_ref,
     col_buf, inv_ref, accept_ref, norm_ref, bonus_ref,
     gs_buf, gq_buf, part_buf,
-    msg2, got1, got2,
+    msg1, msg2, got1, got2,
     send1, recv1, send2, recv2,
 ):
     batch, draft, vocab, ntp = dims
@@ -241,7 +259,6 @@
     barrier = pltpu.get_barrier_semaphore()
     for d in range(1, ntp):
         pl.semaphore_signal(barrier, inc=1, device_id={"tp": lax.rem(me + d, ntp)}, device_id_type=MESH)
-    pl.semaphore_wait(barrier, ntp - 1)
 
     def remote(msg, got, send, recv, d):
         return pltpu.make_async_remote_copy(
@@ -254,19 +271,30 @@
             src_ref=msg, dst_ref=got.at[src], send_sem=send.at[d], recv_sem=recv.at[src],
             device_id={"tp": src}, device_id_type=MESH)
 
+    msg1[...] = jnp.zeros_like(msg1)
+    for g in range(draft + 1):
+        rs = pl.ds(g * batch, batch)
+        m = m_ref[rs, :]
+        top = jnp.max(m, axis=1, keepdims=True)
+        tot = jnp.sum(l_ref[rs, :] * jnp.exp2(m - top), axis=1, keepdims=True)
+        msg1[pl.ds(g, 1), pl.ds(0, batch)] = _col_to_row(top + jnp.log2(tot))
+
+    def token_rows(src, dst):
+        @pl.loop(0, batch, unroll=4)
+        def _(b):
+            for j in range(draft):
+                idx = tok_smem[j, b] - me * vocab
+                idx = jnp.minimum(jnp.maximum(idx, 0), vocab - 1)
+                c = lax.shift_right_logical(idx, 7)
+                dst[pl.ds(j * batch + b, 1), :] = src[c, pl.ds(b * draft + j, 1), :]
+
+    token_rows(q_ref, gq_buf)
+    pl.semaphore_wait(barrier, ntp - 1)
     for d in range(1, ntp):
         remote(msg1, got1, send1, recv1, d).start()
     got1[me] = msg1[...]
 
-    @pl.loop(0, batch)
-    def _(b):
-        for j in range(draft):
-            idx = tok_smem[j, b] - me * vocab
-            idx = jnp.minimum(jnp.maximum(idx, 0), vocab - 1)
-            c = lax.shift_right_logical(idx, 7)
-            gs_buf[pl.ds(j * batch + b, 1), :] = s_ref[c, pl.ds(b * draft + j, 1), :]
-            gq_buf[pl.ds(j * batch + b, 1), :] = q_ref[c, pl.ds(b * draft + j, 1), :]
-
+    token_rows(s_ref, gs_buf)
     msg2[...] = jnp.zeros_like(msg2)
     lane = lax.broadcasted_iota(jnp.int32, (batch, LANES), 1)
     for j in range(draft):
@@ -294,7 +322,6 @@
             _row_to_col(lse2[j:j + 1, 0:batch]), (batch, LANES))
 
     nv = batch * draft // 8
-    unroll = 25 if (nc - 1) % 25 == 0 else 1
     last_mask = lax.broadcasted_iota(jnp.int32, (8, LANES), 1) < last
 
     @pl.loop(0, nv // 2)
@@ -305,16 +332,11 @@
         def ex(c, i):
             return jnp.maximum(jnp.exp2(s_ref[c, rss[i], :] - ls[i]) - q_ref[c, rss[i], :], 0.0)
 
-        def inner(t, sums):
-            sums = list(sums)
-            for u in range(unroll):
-                c = t * unroll + u
-                for i in range(2):
-                    sums[i] = sums[i] + ex(c, i)
-            return tuple(sums)
-
-        zero = jnp.zeros((8, LANES), jnp.float32)
-        sums = lax.fori_loop(0, (nc - 1) // unroll, inner, (zero, zero))
+        sums = [[jnp.zeros((8, LANES), jnp.float32) for _ in range(4)] for _ in range(2)]
+        for c in range(nc - 1):
+            for i in range(2):
+                sums[i][c % 4] = sums[i][c % 4] + ex(c, i)
+        sums = [(a + b) + (c + d) for a, b, c, d in sums]
         for i in range(2):
             e = jnp.where(last_mask, ex(nc - 1, i), 0.0)
             part_buf[rss[i], :] = sums[i] + e
@@ -343,7 +365,6 @@
         remote(msg2, got2, send2, recv2, d).wait_send()
 
 
-OUT_RING = 4
 OUT_GROUP = 5
 
 
@@ -352,46 +373,37 @@
     out_hbm, accept_ref, norm_ref, bonus_ref, stage, stage_last, sem,
 ):
     batch, draft, vocab = dims
+    nc = -(-vocab // LANES)
+    last = vocab - (nc - 1) * LANES
+    view = stage.reshape(nc, batch, draft, LANES)
+    ngroups = (nc - 1) // OUT_GROUP
+    assert ngroups * OUT_GROUP == nc - 1
+
+    def copy(c):
+        return pltpu.make_async_copy(
+            view.at[c], out_hbm.at[:, :, pl.ds(pl.multiple_of(c * LANES, LANES), LANES)], sem.at[0])
+
+    def fill(c):
+        stage[c] = jnp.maximum(jnp.exp2(s_ref[c] - lse_ref[...]) - q_ref[c], 0.0) * inv_ref[...]
+
+    fill(nc - 1)
+    for b in range(batch):
+        stage_last[b] = stage[nc - 1, pl.ds(b * draft, draft), pl.ds(0, last)]
+    last_copy = pltpu.make_async_copy(stage_last, out_hbm.at[:, :, pl.ds((nc - 1) * LANES, last)], sem.at[1])
+    last_copy.start()
+
+    @pl.loop(0, ngroups)
+    def _(t):
+        for i in range(OUT_GROUP):
+            fill(t * OUT_GROUP + i)
+            copy(t * OUT_GROUP + i).start()
+
     accept_ref[...] = accept_in[...]
     norm_ref[...] = norm_in[...]
     bonus_ref[...] = bonus_in[...]
-    nc = -(-vocab // LANES)
-    view = stage.reshape(OUT_RING * OUT_GROUP, batch, draft, LANES)
-    ngroups = (nc - 1) // OUT_GROUP
-    assert ngroups * OUT_GROUP == nc - 1
-
-    def copy(slot, c):
-        return pltpu.make_async_copy(
-            view.at[slot], out_hbm.at[:, :, pl.ds(pl.multiple_of(c * LANES, LANES), LANES)], sem.at[slot])
-
-    def fill(slot, c):
-        stage[slot] = jnp.maximum(jnp.exp2(s_ref[c] - lse_ref[...]) - q_ref[c], 0.0) * inv_ref[...]
-
-    @pl.loop(0, ngroups)
-    def _(t):
-        base = lax.rem(t, OUT_RING) * OUT_GROUP
-
-        @pl.when(t >= OUT_RING)
-        def _():
-            for i in range(OUT_GROUP):
-                copy(base + i, (t - OUT_RING) * OUT_GROUP + i).wait()
-
-        for i in range(OUT_GROUP):
-            fill(base + i, t * OUT_GROUP + i)
-            copy(base + i, t * OUT_GROUP + i).start()
-
-    for t in range(ngroups - OUT_RING, ngroups):
-        for i in range(OUT_GROUP):
-            copy(t % OUT_RING * OUT_GROUP + i, t * OUT_GROUP + i).wait()
-    c = nc - 1
-    last = vocab - c * LANES
-    fill(0, c)
-    for b in range(batch):
-        rs = pl.ds(b * draft, draft)
-        stage_last[b] = stage[0, rs, pl.ds(0, last)]
-    final = pltpu.make_async_copy(stage_last, out_hbm.at[:, :, pl.ds(c * LANES, last)], sem.at[0])
-    final.start()
-    final.wait()
+    last_copy.wait()
+    bulk = stage.at[pl.ds(0, nc - 1)]
+    pltpu.make_async_copy(bulk, bulk, sem.at[0]).wait()
 
 
 def solution(mesh):
@@ -409,24 +421,24 @@
         f32, bf16, dma = jnp.float32, jnp.bfloat16, pltpu.SemaphoreType.DMA
         vec = pltpu.VMEM((batch * draft, LANES), f32)
         big = pltpu.VMEM((nc, batch * draft, LANES), f32)
+        stat = pltpu.VMEM((rows, LANES), f32)
         x = hidden.transpose(1, 0, 2).reshape(rows, depth)
         tok = draft_tokens.T
-        s, q, lse = pl.pallas_call(
+        s, q, m, l = pl.pallas_call(
             functools.partial(_logits_kernel, (batch, draft, depth, vocab)),
-            out_shape=(big, big, pltpu.VMEM((8, LANES), f32)),
+            out_shape=(big, big, stat, stat),
             in_specs=[hbm, vmem, hbm, hbm, vmem],
-            out_specs=(vmem,) * 3,
+            out_specs=(vmem,) * 4,
             scratch_shapes=[
                 pltpu.VMEM((rows, depth), bf16),
                 pltpu.VMEM((rows, depth), bf16),
                 pltpu.VMEM((RING, STEP, depth), bf16),
                 pltpu.VMEM((batch, draft, vocab - (nc - 1) * LANES), f32),
-                pltpu.VMEM((rows, LANES), f32),
-                pltpu.VMEM((rows, LANES), f32),
                 pltpu.VMEM((batch, LANES), f32),
                 dma,
-                dma((RING,)),
-                dma((nc,)),
+                dma((RING, W_PARTS)),
+                dma((2,)),
+                pltpu.SemaphoreType.REGULAR,
             ],
             compiler_params=pltpu.CompilerParams(vmem_limit_bytes=GRANT),
             name="logits",
@@ -440,10 +452,11 @@
                 pltpu.VMEM((draft, batch), f32),
                 pltpu.VMEM((1, batch), f32),
             ),
-            in_specs=[vmem, vmem, vmem, smem, vmem],
+            in_specs=[vmem, vmem, vmem, vmem, smem, vmem],
             out_specs=(vmem,) * 5,
             scratch_shapes=[
                 vec, vec, vec,
+                pltpu.VMEM((8, LANES), f32),
                 pltpu.VMEM((16, LANES), f32),
                 pltpu.VMEM((ntp, 8, LANES), f32),
                 pltpu.VMEM((ntp, 16, LANES), f32),
@@ -452,7 +465,7 @@
             compiler_params=pltpu.CompilerParams(
                 collective_id=0, has_side_effects=True, vmem_limit_bytes=GRANT),
             name="verify",
-        )(keep(s), keep(q), keep(lse), tok, tok)
+        )(keep(s), keep(q), keep(m), keep(l), tok, tok)
         residual, accept, norm, bonus = pl.pallas_call(
             functools.partial(_write_kernel, (batch, draft, vocab)),
             out_shape=(
@@ -464,9 +477,9 @@
             in_specs=[vmem] * 7,
             out_specs=(hbm, vmem, vmem, vmem),
             scratch_shapes=[
-                pltpu.VMEM((OUT_RING * OUT_GROUP, batch * draft, LANES), f32),
+                big,
                 pltpu.VMEM((batch, draft, vocab - (nc - 1) * LANES), f32),
-                dma((OUT_RING * OUT_GROUP,)),
+                dma((2,)),
             ],
             compiler_params=pltpu.CompilerParams(vmem_limit_bytes=GRANT),
             name="write",

time: 58.9 us -> 54.4 us (0.924)
  Pallas kernels: 58.1 us -> 53.6 us
    pallas_call x1, Pallas kernels: 34.1 us -> 30.1 us  [local_step(): pl.pallas_call(functools.partial(_logits_kernel, (batch, draft, depth, vo...]
    pallas_call x1, Pallas kernels: 7.47 us -> 6.29 us  [local_step(): pl.pallas_call(functools.partial(_write_kernel, (batch, draft, vocab)), o...]
where the time goes in v2:
time: 54.4 us; the launch traced here: 54.2 us
  Pallas kernels  53.6 us (99%)
  between operations  0.65 us (1%)
    pallas_call x1, Pallas kernels, local_step(): pl.pallas_call(functools.partial(_logits_kernel, (batch, draft, depth, vo...  30.1 us
    pallas_call x1, Pallas kernels, local_step(): pl.pallas_call(functools.partial(_verify_kernel, (batch, draft, vocab, nt...  17.1 us
    pallas_call x1, Pallas kernels, local_step(): pl.pallas_call(functools.partial(_write_kernel, (batch, draft, vocab)), o...  6.29 us

profile of v2, /device:TPU:81, one launch (start us, length us, event | category | flops | bytes accessed | tf_op | source)
XLA Modules:
  0.0 54.2 jit_solution(7573608063159469808)
XLA Ops:
  0.6 30.1 %logits.1 = (f32[126,256,128]{2,1,0:T(8,128)S(1)}, f32[126,256,128]{2,1,0:T(8,128)S(1)}, f32[320,128]{1,0:T(8,128)S(1)}, f32[320,128]{1,0:T(8,128)S(1)}) custom-call(bf16[320,2048]{1,0:T(8,128)(2,1)} %bitcast.11, f32[1,2048]{1,0:T(1,128)} %bitcast.12, bf16[16032,2048]{1,0:T(8,128)(2,1)} %bitcast.10, f32[64,4,16032]{2,1,0:T(4,128)} %q_hbm.1, f32[1,64]{1,0:T(1,128)} %bitcast.15), custom_call_target="tpu_custom_call" | custom-call | tf_op jit(solution)/shard_map/logits/pallas_call | solution.py:427
  30.8 17.1 %verify.1 = (f32[256,128]{1,0:T(8,128)S(1)}, f32[256,128]{1,0:T(8,128)S(1)}, f32[4,64]{1,0:T(4,128)S(1)}, f32[4,64]{1,0:T(4,128)S(1)}, f32[1,64]{1,0:T(1,128)S(1)}) custom-call(f32[126,256,128]{2,1,0:T(8,128)S(1)} %get-tuple-element.17.s_ref, f32[126,256,128]{2,1,0:T(8,128)S(1)} %get-tuple-element.18.q_ref, f32[320,128]{1,0:T(8,128)S(1)} %get-tuple-element.19.m_ref, ...), custom_call_target="tpu_custom_call" | custom-call | tf_op jit(solution)/shard_map/verify/pallas_call | solution.py:446
  47.9 6.3 %write.1 = (f32[64,4,16032]{2,1,0:T(4,128)}, f32[4,64]{1,0:T(4,128)}, f32[4,64]{1,0:T(4,128)}, f32[1,64]{1,0:T(1,128)}) custom-call(f32[126,256,128]{2,1,0:T(8,128)S(1)} %get-tuple-element.17.s_ref, f32[126,256,128]{2,1,0:T(8,128)S(1)} %get-tuple-element.18.q_ref, f32[256,128]{1,0:T(8,128)S(1)} %get-tuple-element.21.lse_ref, ...), custom_call_target="tpu_custom_call" | custom-call | tf_op jit(solution)/shard_map/write/pallas_call | solution.py:469

commit v3 on v2

--- a/solution.py
+++ b/solution.py
@@ -11,8 +11,12 @@
 TILE = 256
 STEP = 2 * TILE
 RING = 8
+SLAB = 64
+CHUNK = 25
 W_PARTS = 4
 FENCES = 6
+Q_LATE = 5
+TOK_STEP = 8
 SIG = (1, 3, 5, 7)
 GRP = {1: (0,), 3: (1, 2), 5: (3, 4)}
 GRANT = 24 * 1024 * 1024
@@ -36,14 +40,21 @@
     return jnp.sum(jnp.where(r == c, col, 0.0), axis=0, keepdims=True)
 
 
+def _q_first(vocab):
+    return (vocab // LANES) * Q_LATE // 8
+
+
 def _logits_kernel(
     dims,
-    x_hbm, gain_ref, w_hbm, q_hbm, temp_ref,
-    s_ref, q_buf, m_buf, l_buf,
+    x_hbm, gain_ref, w_hbm, q_hbm, temp_ref, tok_smem,
+    s_ref, q_buf, m_buf, l_buf, tile_ref,
     h_buf, x_buf, w_buf, q_last, scale_buf,
     h_sem, w_sem, q_sem, fence,
 ):
     batch, draft, depth, vocab = dims
+    tokens = batch * draft
+    me = lax.axis_index("tp")
+    q_first = _q_first(vocab)
     rows = batch * (draft + 1)
     nk = depth // TILE
     full = vocab // STEP
@@ -64,11 +75,19 @@
     def w_rest():
         return [w_copy(full, i, min(part, rest - i * part)) for i in range(-(-rest // part))]
 
+    tiles = tile_ref.reshape(tokens, draft, LANES)
     qv = q_buf.reshape(nc, batch, draft, LANES)
 
     def q_copy(c):
         return pltpu.make_async_copy(
             q_hbm.at[:, :, pl.ds(pl.multiple_of(c * LANES, LANES), LANES)], qv.at[c], q_sem.at[0])
+
+    def token_copy(b, j):
+        idx = tok_smem[j, b] - me * vocab
+        c = lax.shift_right_logical(jnp.minimum(jnp.maximum(idx, 0), vocab - 1), 7)
+        c = jnp.minimum(c, nc - 2)
+        return pltpu.make_async_copy(
+            q_hbm.at[b, :, pl.ds(pl.multiple_of(c * LANES, LANES), LANES)], tiles.at[b * draft + j], q_sem.at[2])
 
     def last_q():
         return pltpu.make_async_copy(
@@ -167,26 +186,25 @@
 
         split = (full - (RING - 1)) // 2 * 2
         tail = full // 2 * 2
-        early = FENCES - W_PARTS
-        late = 8
-        final = FENCES
-        mid = nc - 1 - early * split - late * (tail - split) - final
-        assert mid >= 0 and tail == full - 1
+        early = 1
+        mid = nc - 1 - q_first - early * split
+        assert mid >= 0 and tail == full - 1 and tokens >= TOK_STEP * full
+
+        def issue_tokens(n):
+            for i in range(TOK_STEP):
+                token_copy(n * (TOK_STEP // draft) + i // draft, i % draft).start(priority=1)
 
         def issue_early(n, i):
             if i < W_PARTS:
                 w_copy(n + RING - 1, i).start()
+            elif i == W_PARTS:
+                q_copy(q_first + n).start(priority=1)
             else:
-                q_copy(n * early + i - W_PARTS).start(priority=1)
+                issue_tokens(n)
 
         def issue_late(n, i):
-            base = early * split + mid + (n - split) * late
-            q_copy(base + i).start(priority=1)
-            if i < late - FENCES:
-                q_copy(base + FENCES + i).start(priority=1)
-
-        def issue_final(i):
-            q_copy(nc - 1 - final + i).start(priority=1)
+            if i == W_PARTS + 1:
+                issue_tokens(n)
 
         @pl.loop(0, split // 2)
         def _(t):
@@ -201,7 +219,10 @@
 
         @pl.loop(0, mid)
         def _(i):
-            q_copy(early * split + i).start(priority=1)
+            q_copy(q_first + early * split + i).start(priority=1)
+
+        for i in range(TOK_STEP * full, tokens):
+            token_copy(i // draft, i % draft).start(priority=1)
 
         @pl.loop(split // 2, tail // 2)
         def _(t):
@@ -217,7 +238,7 @@
         last_q().wait()
         for b in range(0, batch, 2):
             q_buf[nc - 1, pl.ds(b * draft, 2 * draft), pl.ds(0, last)] = jnp.concatenate([q_last[b], q_last[b + 1]], axis=0)
-        fullstep(n, 0, issue_final, next_full=False)
+        fullstep(n, 0, lambda i: issue_late(n, i), next_full=False)
         for kk in range(half):
             for q in range(2):
                 for g in range(groups):
@@ -240,18 +261,20 @@
     specs = [pltpu.ACC(q)((batch, TILE), jnp.float32) for a in range(2) for q in range(2) for g in range(groups)]
     pl.run_scoped(mxu_body, *specs)
 
-    bulk = q_buf.at[pl.ds(0, nc - 1)]
+    bulk = q_buf.at[pl.ds(q_first, nc - 1 - q_first)]
     pltpu.make_async_copy(bulk, bulk, q_sem.at[0]).wait()
+    pltpu.make_async_copy(tile_ref, tile_ref, q_sem.at[2]).wait()
 
 
 def _verify_kernel(
     dims,
-    s_ref, q_ref, m_ref, l_ref, tok_smem, tok_ref,
-    col_buf, inv_ref, accept_ref, norm_ref, bonus_ref,
-    gs_buf, gq_buf, part_buf,
+    s_ref, q_in, m_ref, l_ref, tile_ref, tok_smem, tok_ref, q_hbm,
+    q_ref, col_buf, inv_ref, accept_ref, norm_ref, bonus_ref,
+    gs_buf, part_buf,
     msg1, msg2, got1, got2,
-    send1, recv1, send2, recv2,
+    send1, recv1, send2, recv2, q_sem,
 ):
+    del q_in
     batch, draft, vocab, ntp = dims
     nc = -(-vocab // LANES)
     last = vocab - (nc - 1) * LANES
@@ -259,6 +282,16 @@
     barrier = pltpu.get_barrier_semaphore()
     for d in range(1, ntp):
         pl.semaphore_signal(barrier, inc=1, device_id={"tp": lax.rem(me + d, ntp)}, device_id_type=MESH)
+    q_first = _q_first(vocab)
+    qv = q_ref.reshape(nc, batch, draft, LANES)
+
+    def q_copy(c):
+        return pltpu.make_async_copy(
+            q_hbm.at[:, :, pl.ds(pl.multiple_of(c * LANES, LANES), LANES)], qv.at[c], q_sem.at[c])
+
+    @pl.loop(0, q_first)
+    def _(c):
+        q_copy(c).start()
 
     def remote(msg, got, send, recv, d):
         return pltpu.make_async_remote_copy(
@@ -288,7 +321,6 @@
                 c = lax.shift_right_logical(idx, 7)
                 dst[pl.ds(j * batch + b, 1), :] = src[c, pl.ds(b * draft + j, 1), :]
 
-    token_rows(q_ref, gq_buf)
     pl.semaphore_wait(barrier, ntp - 1)
     for d in range(1, ntp):
         remote(msg1, got1, send1, recv1, d).start()
@@ -303,7 +335,11 @@
         hit = jnp.logical_and(owned, lane == jnp.bitwise_and(idx, LANES - 1))
         rs = pl.ds(j * batch, batch)
         tok_s = jnp.sum(jnp.where(hit, gs_buf[rs, :], 0.0), axis=1, keepdims=True)
-        tok_q = jnp.sum(jnp.where(hit, gq_buf[rs, :], 0.0), axis=1, keepdims=True)
+        q_row = jnp.where(
+            lax.shift_right_logical(idx, 7) == nc - 1,
+            q_ref[nc - 1, pl.ds(j, batch, stride=draft), :],
+            tile_ref[pl.ds((draft + 1) * j, batch, stride=draft * draft), :])
+        tok_q = jnp.sum(jnp.where(hit, q_row, 0.0), axis=1, keepdims=True)
         msg2[pl.ds(draft + j, 1), pl.ds(0, batch)] = _col_to_row(tok_s)
         msg2[pl.ds(2 * draft + j, 1), pl.ds(0, batch)] = _col_to_row(tok_q)
 
@@ -321,25 +357,27 @@
         col_buf[pl.ds(j, batch, stride=draft), :] = jnp.broadcast_to(
             _row_to_col(lse2[j:j + 1, 0:batch]), (batch, LANES))
 
-    nv = batch * draft // 8
-    last_mask = lax.broadcasted_iota(jnp.int32, (8, LANES), 1) < last
-
-    @pl.loop(0, nv // 2)
+    @pl.loop(0, q_first)
+    def _(c):
+        q_copy(c).wait()
+
+    last_mask = lax.broadcasted_iota(jnp.int32, (SLAB, LANES), 1) < last
+
+    @pl.loop(0, batch * draft // SLAB)
     def _(v):
-        rss = [pl.ds(pl.multiple_of((2 * v + i) * 8, 8), 8) for i in range(2)]
-        ls = [col_buf[rs, :] for rs in rss]
-
-        def ex(c, i):
-            return jnp.maximum(jnp.exp2(s_ref[c, rss[i], :] - ls[i]) - q_ref[c, rss[i], :], 0.0)
-
-        sums = [[jnp.zeros((8, LANES), jnp.float32) for _ in range(4)] for _ in range(2)]
-        for c in range(nc - 1):
-            for i in range(2):
-                sums[i][c % 4] = sums[i][c % 4] + ex(c, i)
-        sums = [(a + b) + (c + d) for a, b, c, d in sums]
-        for i in range(2):
-            e = jnp.where(last_mask, ex(nc - 1, i), 0.0)
-            part_buf[rss[i], :] = sums[i] + e
+        rs = pl.ds(pl.multiple_of(v * SLAB, SLAB), SLAB)
+        lse = col_buf[rs, :]
+
+        def ex(c):
+            return jnp.maximum(jnp.exp2(s_ref[c, rs, :] - lse) - q_ref[c, rs, :], 0.0)
+
+        def chunk(t, total):
+            for i in range(CHUNK):
+                total = total + ex(t * CHUNK + i)
+            return total
+
+        part_buf[rs, :] = lax.fori_loop(
+            0, (nc - 1) // CHUNK, chunk, jnp.where(last_mask, ex(nc - 1), 0.0))
 
     for j in range(draft):
         part = jnp.sum(part_buf[pl.ds(j, batch, stride=draft), :], axis=1, keepdims=True)
@@ -424,11 +462,11 @@
         stat = pltpu.VMEM((rows, LANES), f32)
         x = hidden.transpose(1, 0, 2).reshape(rows, depth)
         tok = draft_tokens.T
-        s, q, m, l = pl.pallas_call(
+        s, q, m, l, tiles = pl.pallas_call(
             functools.partial(_logits_kernel, (batch, draft, depth, vocab)),
-            out_shape=(big, big, stat, stat),
-            in_specs=[hbm, vmem, hbm, hbm, vmem],
-            out_specs=(vmem,) * 4,
+            out_shape=(big, big, stat, stat, pltpu.VMEM((batch * draft * draft, LANES), f32)),
+            in_specs=[hbm, vmem, hbm, hbm, vmem, smem],
+            out_specs=(vmem,) * 5,
             scratch_shapes=[
                 pltpu.VMEM((rows, depth), bf16),
                 pltpu.VMEM((rows, depth), bf16),
@@ -437,35 +475,37 @@
                 pltpu.VMEM((batch, LANES), f32),
                 dma,
                 dma((RING, W_PARTS)),
-                dma((2,)),
+                dma((3,)),
                 pltpu.SemaphoreType.REGULAR,
             ],
             compiler_params=pltpu.CompilerParams(vmem_limit_bytes=GRANT),
             name="logits",
-        )(x, norm_gain.reshape(1, depth), w_head.T, draft_probs, temperature.reshape(1, batch))
-        lse, inv, accept, norm, bonus = pl.pallas_call(
+        )(x, norm_gain.reshape(1, depth), w_head.T, draft_probs, temperature.reshape(1, batch), tok)
+        q, lse, inv, accept, norm, bonus = pl.pallas_call(
             functools.partial(_verify_kernel, (batch, draft, vocab, ntp)),
             out_shape=(
+                big,
                 vec,
                 vec,
                 pltpu.VMEM((draft, batch), f32),
                 pltpu.VMEM((draft, batch), f32),
                 pltpu.VMEM((1, batch), f32),
             ),
-            in_specs=[vmem, vmem, vmem, vmem, smem, vmem],
-            out_specs=(vmem,) * 5,
+            in_specs=[vmem, vmem, vmem, vmem, vmem, smem, vmem, hbm],
+            out_specs=(vmem,) * 6,
+            input_output_aliases={1: 0},
             scratch_shapes=[
-                vec, vec, vec,
+                vec, vec,
                 pltpu.VMEM((8, LANES), f32),
                 pltpu.VMEM((16, LANES), f32),
                 pltpu.VMEM((ntp, 8, LANES), f32),
                 pltpu.VMEM((ntp, 16, LANES), f32),
-                dma((ntp,)), dma((ntp,)), dma((ntp,)), dma((ntp,)),
+                dma((ntp,)), dma((ntp,)), dma((ntp,)), dma((ntp,)), dma((nc,)),
             ],
             compiler_params=pltpu.CompilerParams(
                 collective_id=0, has_side_effects=True, vmem_limit_bytes=GRANT),
             name="verify",
-        )(keep(s), keep(q), keep(m), keep(l), tok, tok)
+        )(keep(s), keep(q), keep(m), keep(l), keep(tiles), tok, tok, draft_probs)
         residual, accept, norm, bonus = pl.pallas_call(
             functools.partial(_write_kernel, (batch, draft, vocab)),
             out_shape=(

time: 54.4 us -> 54.8 us (level)
  no operation moved by 1% of the time
where the time goes in v3:
time: 54.8 us; the launch traced here: 54.5 us
  Pallas kernels  53.9 us (98%)
  between operations  0.65 us (1%)
    pallas_call x1, Pallas kernels, local_step(): pl.pallas_call(functools.partial(_logits_kernel, (batch, draft, depth, vo...  30.2 us
    pallas_call x1, Pallas kernels, local_step(): pl.pallas_call(functools.partial(_verify_kernel, (batch, draft, vocab, nt...  17.4 us
    pallas_call x1, Pallas kernels, local_step(): pl.pallas_call(functools.partial(_write_kernel, (batch, draft, vocab)), o...  6.29 us

profile of v3, /device:TPU:81, one launch (start us, length us, event | category | flops | bytes accessed | tf_op | source)
XLA Modules:
  0.0 54.5 jit_solution(6492501615842860801)
XLA Ops:
  0.6 30.2 %logits.1 = (f32[126,256,128]{2,1,0:T(8,128)S(1)}, f32[126,256,128]{2,1,0:T(8,128)S(1)}, f32[320,128]{1,0:T(8,128)S(1)}, f32[320,128]{1,0:T(8,128)S(1)}, f32[1024,128]{1,0:T(8,128)S(1)}) custom-call(bf16[320,2048]{1,0:T(8,128)(2,1)} %bitcast.11, f32[1,2048]{1,0:T(1,128)} %bitcast.15, bf16[16032,2048]{1,0:T(8,128)(2,1)} %bitcast.10, f32[64,4,16032]{2,1,0:T(4,128)} %q_hbm.3, ...), custom_call_target="tpu_custom_call" | custom-call | tf_op jit(solution)/shard_map/logits/pallas_call | solution.py:465
  30.8 17.4 %verify.1 = (f32[126,256,128]{2,1,0:T(8,128)S(1)}, f32[256,128]{1,0:T(8,128)S(1)}, f32[256,128]{1,0:T(8,128)S(1)}, f32[4,64]{1,0:T(4,128)S(1)}, f32[4,64]{1,0:T(4,128)S(1)}, /*index=5*/f32[1,64]{1,0:T(1,128)S(1)}) custom-call(f32[126,256,128]{2,1,0:T(8,128)S(1)} %get-tuple-element.19.s_ref, ...), custom_call_target="tpu_custom_call", output_to_operand_aliasing={{0}: (1, {})} | custom-call | tf_op jit(solution)/shard_map/verify/pallas_call | solution.py:484
  48.2 6.3 %write.1 = (f32[64,4,16032]{2,1,0:T(4,128)}, f32[4,64]{1,0:T(4,128)}, f32[4,64]{1,0:T(4,128)}, f32[1,64]{1,0:T(1,128)}) custom-call(f32[126,256,128]{2,1,0:T(8,128)S(1)} %get-tuple-element.19.s_ref, f32[126,256,128]{2,1,0:T(8,128)S(1)} %get-tuple-element.24.q_ref, f32[256,128]{1,0:T(8,128)S(1)} %get-tuple-element.25.lse_ref, ...), custom_call_target="tpu_custom_call" | custom-call | tf_op jit(solution)/shard_map/write/pallas_call | solution.py:509

commit v4 on v3

--- a/solution.py
+++ b/solution.py
@@ -46,10 +46,10 @@
 
 def _logits_kernel(
     dims,
-    x_hbm, gain_ref, w_hbm, q_hbm, temp_ref, tok_smem,
+    x_hbm, gain_hbm, w_hbm, q_hbm, temp_hbm, tok_hbm,
     s_ref, q_buf, m_buf, l_buf, tile_ref,
-    h_buf, x_buf, w_buf, q_last, scale_buf,
-    h_sem, w_sem, q_sem, fence,
+    h_buf, x_buf, w_buf, q_last, scale_buf, gain_ref, temp_ref, tok_smem,
+    h_sem, w_sem, q_sem, small_sem, fence,
 ):
     batch, draft, depth, vocab = dims
     tokens = batch * draft
@@ -93,15 +93,23 @@
         return pltpu.make_async_copy(
             q_hbm.at[:, :, pl.ds((nc - 1) * LANES, last)], q_last, q_sem.at[1])
 
-    h_copy = pltpu.make_async_copy(x_hbm, h_buf, h_sem)
-    h_copy.start()
+    def h_copy(g):
+        rs = pl.ds(g * batch, batch)
+        return pltpu.make_async_copy(x_hbm.at[rs, :], h_buf.at[rs, :], h_sem.at[g])
+
+    small = [
+        pltpu.make_async_copy(src, dst, small_sem.at[i])
+        for i, (src, dst) in enumerate([(gain_hbm, gain_ref), (temp_hbm, temp_ref), (tok_hbm, tok_smem)])
+    ]
+    for g in range(draft + 1):
+        h_copy(g).start()
+    for copy in small:
+        copy.start()
     for n in range(RING - 1):
         for i in range(W_PARTS):
-            w_copy(n, i).start()
+            w_copy(n, i).start(priority=i % 2)
     last_q().start(priority=1)
 
-    temp_col = _row_to_col(temp_ref[...])
-    scale_buf[...] = jnp.broadcast_to(LOG2E / temp_col, (batch, LANES))
     m_buf[...] = jnp.full_like(m_buf, LOWEST)
     l_buf[...] = jnp.zeros_like(l_buf)
 
@@ -141,7 +149,11 @@
                 for g in range(groups):
                     pltpu.matmul_pop(acc[a][q][g])
 
-        h_copy.wait()
+        for copy in small:
+            copy.wait()
+        scale_buf[...] = jnp.broadcast_to(LOG2E / _row_to_col(temp_ref[...]), (batch, LANES))
+        for g in range(draft + 1):
+            h_copy(g).wait()
         for i in range(rows // 32):
             sl = pl.ds(i * 32, 32)
             h = h_buf[sl, :].astype(jnp.float32)
@@ -196,7 +208,7 @@
 
         def issue_early(n, i):
             if i < W_PARTS:
-                w_copy(n + RING - 1, i).start()
+                w_copy(n + RING - 1, i).start(priority=i % 2)
             elif i == W_PARTS:
                 q_copy(q_first + n).start(priority=1)
             else:
@@ -214,8 +226,8 @@
             w_wait(n + 2)
             fullstep(n + 1, 1, lambda i: issue_early(n + 1, i))
 
-        for copy in w_rest():
-            copy.start()
+        for i, copy in enumerate(w_rest()):
+            copy.start(priority=i % 2)
 
         @pl.loop(0, mid)
         def _(i):
@@ -268,11 +280,11 @@
 
 def _verify_kernel(
     dims,
-    s_ref, q_in, m_ref, l_ref, tile_ref, tok_smem, tok_ref, q_hbm,
+    s_ref, q_in, m_ref, l_ref, tile_ref, tok_hbm, q_hbm,
     q_ref, col_buf, inv_ref, accept_ref, norm_ref, bonus_ref,
-    gs_buf, part_buf,
+    gs_buf, part_buf, tok_smem, tok_ref,
     msg1, msg2, got1, got2,
-    send1, recv1, send2, recv2, q_sem,
+    send1, recv1, send2, recv2, q_sem, tok_sem,
 ):
     del q_in
     batch, draft, vocab, ntp = dims
@@ -289,6 +301,13 @@
         return pltpu.make_async_copy(
             q_hbm.at[:, :, pl.ds(pl.multiple_of(c * LANES, LANES), LANES)], qv.at[c], q_sem.at[c])
 
+    tok_copies = [
+        pltpu.make_async_copy(tok_hbm, tok_smem, tok_sem.at[0]),
+        pltpu.make_async_copy(tok_hbm, tok_ref, tok_sem.at[1]),
+    ]
+    for copy in tok_copies:
+        copy.start()
+
     @pl.loop(0, q_first)
     def _(c):
         q_copy(c).start()
@@ -326,6 +345,8 @@
         remote(msg1, got1, send1, recv1, d).start()
     got1[me] = msg1[...]
 
+    for copy in tok_copies:
+        copy.wait()
     token_rows(s_ref, gs_buf)
     msg2[...] = jnp.zeros_like(msg2)
     lane = lax.broadcasted_iota(jnp.int32, (batch, LANES), 1)
@@ -417,13 +438,19 @@
     ngroups = (nc - 1) // OUT_GROUP
     assert ngroups * OUT_GROUP == nc - 1
 
-    def copy(c):
+    def out_copy(c):
         return pltpu.make_async_copy(
             view.at[c], out_hbm.at[:, :, pl.ds(pl.multiple_of(c * LANES, LANES), LANES)], sem.at[0])
 
     def fill(c):
         stage[c] = jnp.maximum(jnp.exp2(s_ref[c] - lse_ref[...]) - q_ref[c], 0.0) * inv_ref[...]
 
+    small = [
+        pltpu.make_async_copy(src, dst, sem.at[2 + i])
+        for i, (src, dst) in enumerate([(accept_in, accept_ref), (norm_in, norm_ref), (bonus_in, bonus_ref)])
+    ]
+    for copy in small:
+        copy.start()
     fill(nc - 1)
     for b in range(batch):
         stage_last[b] = stage[nc - 1, pl.ds(b * draft, draft), pl.ds(0, last)]
@@ -434,12 +461,11 @@
     def _(t):
         for i in range(OUT_GROUP):
             fill(t * OUT_GROUP + i)
-            copy(t * OUT_GROUP + i).start()
-
-    accept_ref[...] = accept_in[...]
-    norm_ref[...] = norm_in[...]
-    bonus_ref[...] = bonus_in[...]
+            out_copy(t * OUT_GROUP + i).start()
+
     last_copy.wait()
+    for copy in small:
+        copy.wait()
     bulk = stage.at[pl.ds(0, nc - 1)]
     pltpu.make_async_copy(bulk, bulk, sem.at[0]).wait()
 
@@ -454,7 +480,6 @@
         nc = -(-vocab // LANES)
         vmem = pl.BlockSpec(memory_space=pltpu.VMEM)
         hbm = pl.BlockSpec(memory_space=pl.ANY)
-        smem = pl.BlockSpec(memory_space=pltpu.SMEM)
         keep = functools.partial(pltpu.with_memory_space_constraint, memory_space=pltpu.VMEM)
         f32, bf16, dma = jnp.float32, jnp.bfloat16, pltpu.SemaphoreType.DMA
         vec = pltpu.VMEM((batch * draft, LANES), f32)
@@ -465,7 +490,7 @@
         s, q, m, l, tiles = pl.pallas_call(
             functools.partial(_logits_kernel, (batch, draft, depth, vocab)),
             out_shape=(big, big, stat, stat, pltpu.VMEM((batch * draft * draft, LANES), f32)),
-            in_specs=[hbm, vmem, hbm, hbm, vmem, smem],
+            in_specs=[hbm] * 6,
             out_specs=(vmem,) * 5,
             scratch_shapes=[
                 pltpu.VMEM((rows, depth), bf16),
@@ -473,8 +498,12 @@
                 pltpu.VMEM((RING, STEP, depth), bf16),
                 pltpu.VMEM((batch, draft, vocab - (nc - 1) * LANES), f32),
                 pltpu.VMEM((batch, LANES), f32),
-                dma,
+                pltpu.VMEM((1, depth), f32),
+                pltpu.VMEM((1, batch), f32),
+                pltpu.SMEM((draft, batch), jnp.int32),
+                dma((draft + 1,)),
                 dma((RING, W_PARTS)),
+                dma((3,)),
                 dma((3,)),
                 pltpu.SemaphoreType.REGULAR,
             ],
@@ -491,21 +520,23 @@
                 pltpu.VMEM((draft, batch), f32),
                 pltpu.VMEM((1, batch), f32),
             ),
-            in_specs=[vmem, vmem, vmem, vmem, vmem, smem, vmem, hbm],
+            in_specs=[vmem, vmem, vmem, vmem, vmem, hbm, hbm],
             out_specs=(vmem,) * 6,
             input_output_aliases={1: 0},
             scratch_shapes=[
                 vec, vec,
+                pltpu.SMEM((draft, batch), jnp.int32),
+                pltpu.VMEM((draft, batch), jnp.int32),
                 pltpu.VMEM((8, LANES), f32),
                 pltpu.VMEM((16, LANES), f32),
                 pltpu.VMEM((ntp, 8, LANES), f32),
                 pltpu.VMEM((ntp, 16, LANES), f32),
-                dma((ntp,)), dma((ntp,)), dma((ntp,)), dma((ntp,)), dma((nc,)),
+                dma((ntp,)), dma((ntp,)), dma((ntp,)), dma((ntp,)), dma((nc,)), dma((2,)),
             ],
             compiler_params=pltpu.CompilerParams(
                 collective_id=0, has_side_effects=True, vmem_limit_bytes=GRANT),
             name="verify",
-        )(keep(s), keep(q), keep(m), keep(l), keep(tiles), tok, tok, draft_probs)
+        )(keep(s), keep(q), keep(m), keep(l), keep(tiles), tok, draft_probs)
         residual, accept, norm, bonus = pl.pallas_call(
             functools.partial(_write_kernel, (batch, draft, vocab)),
             out_shape=(
@@ -515,11 +546,11 @@
                 jax.ShapeDtypeStruct((1, batch), f32),
             ),
             in_specs=[vmem] * 7,
-            out_specs=(hbm, vmem, vmem, vmem),
+            out_specs=(hbm,) * 4,
             scratch_shapes=[
                 big,
                 pltpu.VMEM((batch, draft, vocab - (nc - 1) * LANES), f32),
-                dma((2,)),
+                dma((5,)),
             ],
             compiler_params=pltpu.CompilerParams(vmem_limit_bytes=GRANT),
             name="write",

time: 54.8 us -> 50.7 us (0.925)
  Pallas kernels: 53.9 us -> 49.9 us
    pallas_call x1, Pallas kernels: 30.2 us -> 27.5 us  [local_step(): pl.pallas_call(functools.partial(_logits_kernel, (batch, draft, depth, vo...]
    pallas_call x1, Pallas kernels: 17.4 us -> 16.7 us  [local_step(): pl.pallas_call(functools.partial(_verify_kernel, (batch, draft, vocab, nt...]
    pallas_call x1, Pallas kernels: 6.29 us -> 5.74 us  [local_step(): pl.pallas_call(functools.partial(_write_kernel, (batch, draft, vocab)), o...]
where the time goes in v4:
time: 50.7 us; the launch traced here: 50.6 us
  Pallas kernels  49.9 us (98%)
  between operations  0.65 us (1%)
    pallas_call x1, Pallas kernels, local_step(): pl.pallas_call(functools.partial(_logits_kernel, (batch, draft, depth, vo...  27.5 us
    pallas_call x1, Pallas kernels, local_step(): pl.pallas_call(functools.partial(_verify_kernel, (batch, draft, vocab, nt...  16.7 us
    pallas_call x1, Pallas kernels, local_step(): pl.pallas_call(functools.partial(_write_kernel, (batch, draft, vocab)), o...  5.74 us

profile of v4, /device:TPU:81, one launch (start us, length us, event | category | flops | bytes accessed | tf_op | source)
XLA Modules:
  0.0 50.6 jit_solution(7161036072209844621)
XLA Ops:
  0.6 27.5 %logits.1 = (f32[126,256,128]{2,1,0:T(8,128)S(1)}, f32[126,256,128]{2,1,0:T(8,128)S(1)}, f32[320,128]{1,0:T(8,128)S(1)}, f32[320,128]{1,0:T(8,128)S(1)}, f32[1024,128]{1,0:T(8,128)S(1)}) custom-call(bf16[320,2048]{1,0:T(8,128)(2,1)} %bitcast.11, f32[1,2048]{1,0:T(1,128)} %bitcast.12, bf16[16032,2048]{1,0:T(8,128)(2,1)} %bitcast.10, f32[64,4,16032]{2,1,0:T(4,128)} %q_hbm.3, ...), custom_call_target="tpu_custom_call" | custom-call | tf_op jit(solution)/shard_map/logits/pallas_call | solution.py:490
  28.1 16.7 %verify.1 = (f32[126,256,128]{2,1,0:T(8,128)S(1)}, f32[256,128]{1,0:T(8,128)S(1)}, f32[256,128]{1,0:T(8,128)S(1)}, f32[4,64]{1,0:T(4,128)S(1)}, f32[4,64]{1,0:T(4,128)S(1)}, /*index=5*/f32[1,64]{1,0:T(1,128)S(1)}) custom-call(f32[126,256,128]{2,1,0:T(8,128)S(1)} %get-tuple-element.19.s_ref, ...), custom_call_target="tpu_custom_call", output_to_operand_aliasing={{0}: (1, {})} | custom-call | tf_op jit(solution)/shard_map/verify/pallas_call | solution.py:513
  44.8 5.7 %write.1 = (f32[64,4,16032]{2,1,0:T(4,128)}, f32[4,64]{1,0:T(4,128)}, f32[4,64]{1,0:T(4,128)}, f32[1,64]{1,0:T(1,128)}) custom-call(f32[126,256,128]{2,1,0:T(8,128)S(1)} %get-tuple-element.19.s_ref, f32[126,256,128]{2,1,0:T(8,128)S(1)} %get-tuple-element.24.q_ref, f32[256,128]{1,0:T(8,128)S(1)} %get-tuple-element.25.lse_ref, ...), custom_call_target="tpu_custom_call" | custom-call | tf_op jit(solution)/shard_map/write/pallas_call | solution.py:540

commit v5 on v4

--- a/solution.py
+++ b/solution.py
@@ -10,16 +10,16 @@
 LANES = 128
 TILE = 256
 STEP = 2 * TILE
-RING = 8
+RING = 10
 SLAB = 64
 CHUNK = 25
-W_PARTS = 4
+W_PARTS = 2
 FENCES = 6
-Q_LATE = 5
+Q_LATE = 4
 TOK_STEP = 8
 SIG = (1, 3, 5, 7)
 GRP = {1: (0,), 3: (1, 2), 5: (3, 4)}
-GRANT = 24 * 1024 * 1024
+GRANT = 26 * 1024 * 1024
 LOG2E = 1.4426950408889634
 LN2 = 0.6931471805599453
 LOWEST = -3.4028234e38
@@ -211,7 +211,7 @@
                 w_copy(n + RING - 1, i).start(priority=i % 2)
             elif i == W_PARTS:
                 q_copy(q_first + n).start(priority=1)
-            else:
+            elif i == W_PARTS + 1:
                 issue_tokens(n)
 
         def issue_late(n, i):
@@ -308,10 +308,6 @@
     for copy in tok_copies:
         copy.start()
 
-    @pl.loop(0, q_first)
-    def _(c):
-        q_copy(c).start()
-
     def remote(msg, got, send, recv, d):
         return pltpu.make_async_remote_copy(
             src_ref=msg, dst_ref=got.at[me], send_sem=send.at[d], recv_sem=recv.at[me],
@@ -332,7 +328,7 @@
         msg1[pl.ds(g, 1), pl.ds(0, batch)] = _col_to_row(top + jnp.log2(tot))
 
     def token_rows(src, dst):
-        @pl.loop(0, batch, unroll=4)
+        @pl.loop(0, batch, unroll=8)
         def _(b):
             for j in range(draft):
                 idx = tok_smem[j, b] - me * vocab
@@ -344,6 +340,10 @@
     for d in range(1, ntp):
         remote(msg1, got1, send1, recv1, d).start()
     got1[me] = msg1[...]
+
+    @pl.loop(0, q_first)
+    def _(c):
+        q_copy(c).start()
 
     for copy in tok_copies:
         copy.wait()

time: 50.7 us -> 50.5 us (level)
  no operation moved by 1% of the time
where the time goes in v5:
time: 50.5 us; the launch traced here: 50.4 us
  Pallas kernels  49.8 us (99%)
  between operations  0.65 us (1%)
    pallas_call x1, Pallas kernels, local_step(): pl.pallas_call(functools.partial(_logits_kernel, (batch, draft, depth, vo...  27.4 us
    pallas_call x1, Pallas kernels, local_step(): pl.pallas_call(functools.partial(_verify_kernel, (batch, draft, vocab, nt...  16.6 us
    pallas_call x1, Pallas kernels, local_step(): pl.pallas_call(functools.partial(_write_kernel, (batch, draft, vocab)), o...  5.74 us

profile of v5, /device:TPU:81, one launch (start us, length us, event | category | flops | bytes accessed | tf_op | source)
XLA Modules:
  0.0 50.4 jit_solution(6669880563611013443)
XLA Ops:
  0.6 27.4 %logits.1 = (f32[126,256,128]{2,1,0:T(8,128)S(1)}, f32[126,256,128]{2,1,0:T(8,128)S(1)}, f32[320,128]{1,0:T(8,128)S(1)}, f32[320,128]{1,0:T(8,128)S(1)}, f32[1024,128]{1,0:T(8,128)S(1)}) custom-call(bf16[320,2048]{1,0:T(8,128)(2,1)} %bitcast.11, f32[1,2048]{1,0:T(1,128)} %bitcast.12, bf16[16032,2048]{1,0:T(8,128)(2,1)} %bitcast.10, f32[64,4,16032]{2,1,0:T(4,128)} %q_hbm.3, ...), custom_call_target="tpu_custom_call" | custom-call | tf_op jit(solution)/shard_map/logits/pallas_call | solution.py:490
  28.0 16.6 %verify.1 = (f32[126,256,128]{2,1,0:T(8,128)S(1)}, f32[256,128]{1,0:T(8,128)S(1)}, f32[256,128]{1,0:T(8,128)S(1)}, f32[4,64]{1,0:T(4,128)S(1)}, f32[4,64]{1,0:T(4,128)S(1)}, /*index=5*/f32[1,64]{1,0:T(1,128)S(1)}) custom-call(f32[126,256,128]{2,1,0:T(8,128)S(1)} %get-tuple-element.19.s_ref, ...), custom_call_target="tpu_custom_call", output_to_operand_aliasing={{0}: (1, {})} | custom-call | tf_op jit(solution)/shard_map/verify/pallas_call | solution.py:513
  44.7 5.7 %write.1 = (f32[64,4,16032]{2,1,0:T(4,128)}, f32[4,64]{1,0:T(4,128)}, f32[4,64]{1,0:T(4,128)}, f32[1,64]{1,0:T(1,128)}) custom-call(f32[126,256,128]{2,1,0:T(8,128)S(1)} %get-tuple-element.19.s_ref, f32[126,256,128]{2,1,0:T(8,128)S(1)} %get-tuple-element.24.q_ref, f32[256,128]{1,0:T(8,128)S(1)} %get-tuple-element.25.lse_ref, ...), custom_call_target="tpu_custom_call" | custom-call | tf_op jit(solution)/shard_map/write/pallas_call | solution.py:540

commit v6 on v5

--- a/solution.py
+++ b/solution.py
@@ -95,7 +95,7 @@
 
     def h_copy(g):
         rs = pl.ds(g * batch, batch)
-        return pltpu.make_async_copy(x_hbm.at[rs, :], h_buf.at[rs, :], h_sem.at[g])
+        return pltpu.make_async_copy(x_hbm.at[rs, :], h_buf.at[rs, :], h_sem)
 
     small = [
         pltpu.make_async_copy(src, dst, small_sem.at[i])
@@ -299,7 +299,7 @@
 
     def q_copy(c):
         return pltpu.make_async_copy(
-            q_hbm.at[:, :, pl.ds(pl.multiple_of(c * LANES, LANES), LANES)], qv.at[c], q_sem.at[c])
+            q_hbm.at[:, :, pl.ds(pl.multiple_of(c * LANES, LANES), LANES)], qv.at[c], q_sem)
 
     tok_copies = [
         pltpu.make_async_copy(tok_hbm, tok_smem, tok_sem.at[0]),
@@ -337,7 +337,8 @@
                 dst[pl.ds(j * batch + b, 1), :] = src[c, pl.ds(b * draft + j, 1), :]
 
     pl.semaphore_wait(barrier, ntp - 1)
-    for d in range(1, ntp):
+    order = sorted(range(1, ntp), key=lambda d: abs(d - ntp // 2))
+    for d in order:
         remote(msg1, got1, send1, recv1, d).start()
     got1[me] = msg1[...]
 
@@ -364,6 +365,9 @@
         msg2[pl.ds(draft + j, 1), pl.ds(0, batch)] = _col_to_row(tok_s)
         msg2[pl.ds(2 * draft + j, 1), pl.ds(0, batch)] = _col_to_row(tok_q)
 
+    bulk = q_ref.at[pl.ds(0, q_first)]
+    pltpu.make_async_copy(bulk, bulk, q_sem).wait()
+
     for d in range(1, ntp):
         arrived(msg1, got1, send1, recv1, d).wait_recv()
     top = got1[0]
@@ -378,10 +382,6 @@
         col_buf[pl.ds(j, batch, stride=draft), :] = jnp.broadcast_to(
             _row_to_col(lse2[j:j + 1, 0:batch]), (batch, LANES))
 
-    @pl.loop(0, q_first)
-    def _(c):
-        q_copy(c).wait()
-
     last_mask = lax.broadcasted_iota(jnp.int32, (SLAB, LANES), 1) < last
 
     @pl.loop(0, batch * draft // SLAB)
@@ -400,11 +400,10 @@
         part_buf[rs, :] = lax.fori_loop(
             0, (nc - 1) // CHUNK, chunk, jnp.where(last_mask, ex(nc - 1), 0.0))
 
-    for j in range(draft):
-        part = jnp.sum(part_buf[pl.ds(j, batch, stride=draft), :], axis=1, keepdims=True)
-        msg2[pl.ds(j, 1), pl.ds(0, batch)] = _col_to_row(part)
-
-    for d in range(1, ntp):
+    for h in range(batch * draft // LANES):
+        msg2[pl.ds(h, 1), :] = jnp.sum(part_buf[pl.ds(h * LANES, LANES), :].T, axis=0, keepdims=True)
+
+    for d in order:
         remote(msg2, got2, send2, recv2, d).start()
     got2[me] = msg2[...]
     for d in range(1, ntp):
@@ -412,13 +411,12 @@
     tot = got2[0]
     for i in range(1, ntp):
         tot = tot + got2[i]
-    norm = tot[0:draft, 0:batch]
-    norm_ref[...] = norm
+    norm_ref[...] = tot[0:draft, :]
+    inv = 1.0 / tot[0:draft, :]
+    for h in range(batch * draft // LANES):
+        inv_ref[pl.ds(h * LANES, LANES), :] = jnp.broadcast_to(inv[h:h + 1, :], (LANES, LANES)).T
     target = jnp.exp2(tot[draft:2 * draft, 0:batch] - lse2[0:draft, 0:batch])
     accept_ref[...] = jnp.minimum(1.0, target / tot[2 * draft:3 * draft, 0:batch])
-    for j in range(draft):
-        inv_ref[pl.ds(j, batch, stride=draft), :] = jnp.broadcast_to(
-            1.0 / _row_to_col(norm[j:j + 1, :]), (batch, LANES))
     for d in range(1, ntp):
         remote(msg1, got1, send1, recv1, d).wait_send()
         remote(msg2, got2, send2, recv2, d).wait_send()
@@ -429,7 +427,7 @@
 
 def _write_kernel(
     dims, s_ref, q_ref, lse_ref, inv_ref, accept_in, norm_in, bonus_in,
-    out_hbm, accept_ref, norm_ref, bonus_ref, stage, stage_last, sem,
+    out_hbm, accept_ref, norm_ref, bonus_ref, stage, stage_last, norm_col, norm_out, sem,
 ):
     batch, draft, vocab = dims
     nc = -(-vocab // LANES)
@@ -447,10 +445,8 @@
 
     small = [
         pltpu.make_async_copy(src, dst, sem.at[2 + i])
-        for i, (src, dst) in enumerate([(accept_in, accept_ref), (norm_in, norm_ref), (bonus_in, bonus_ref)])
+        for i, (src, dst) in enumerate([(accept_in, accept_ref), (norm_out, norm_ref), (bonus_in, bonus_ref)])
     ]
-    for copy in small:
-        copy.start()
     fill(nc - 1)
     for b in range(batch):
         stage_last[b] = stage[nc - 1, pl.ds(b * draft, draft), pl.ds(0, last)]
@@ -463,7 +459,13 @@
             fill(t * OUT_GROUP + i)
             out_copy(t * OUT_GROUP + i).start()
 
+    for h in range(batch * draft // LANES):
+        norm_col[pl.ds(h * LANES, LANES), :] = jnp.broadcast_to(norm_in[pl.ds(h, 1), :], (LANES, LANES)).T
+    for j in range(draft):
+        norm_out[pl.ds(j, 1), :] = _col_to_row(norm_col[pl.ds(j, batch, stride=draft), pl.ds(0, 1)])
     last_copy.wait()
+    for copy in small:
+        copy.start()
     for copy in small:
         copy.wait()
     bulk = stage.at[pl.ds(0, nc - 1)]
@@ -501,7 +503,7 @@
                 pltpu.VMEM((1, depth), f32),
                 pltpu.VMEM((1, batch), f32),
                 pltpu.SMEM((draft, batch), jnp.int32),
-                dma((draft + 1,)),
+                dma,
                 dma((RING, W_PARTS)),
                 dma((3,)),
                 dma((3,)),
@@ -517,7 +519,7 @@
                 vec,
                 vec,
                 pltpu.VMEM((draft, batch), f32),
-                pltpu.VMEM((draft, batch), f32),
+                pltpu.VMEM((draft, LANES), f32),
                 pltpu.VMEM((1, batch), f32),
             ),
             in_specs=[vmem, vmem, vmem, vmem, vmem, hbm, hbm],
@@ -531,7 +533,7 @@
                 pltpu.VMEM((16, LANES), f32),
                 pltpu.VMEM((ntp, 8, LANES), f32),
                 pltpu.VMEM((ntp, 16, LANES), f32),
-                dma((ntp,)), dma((ntp,)), dma((ntp,)), dma((ntp,)), dma((nc,)), dma((2,)),
+                dma((ntp,)), dma((ntp,)), dma((ntp,)), dma((ntp,)), dma, dma((2,)),
             ],
             compiler_params=pltpu.CompilerParams(
                 collective_id=0, has_side_effects=True, vmem_limit_bytes=GRANT),
@@ -550,6 +552,8 @@
             scratch_shapes=[
                 big,
                 pltpu.VMEM((batch, draft, vocab - (nc - 1) * LANES), f32),
+                vec,
+                pltpu.VMEM((draft, batch), f32),
                 dma((5,)),
             ],
             compiler_params=pltpu.CompilerParams(vmem_limit_bytes=GRANT),

time: 50.5 us -> 48.7 us (0.964)
  Pallas kernels: 49.8 us -> 47.9 us
    pallas_call x1, Pallas kernels: 16.6 us -> 14.8 us  [local_step(): pl.pallas_call(functools.partial(_verify_kernel, (batch, draft, vocab, nt...]
where the time goes in v6:
time: 48.7 us; the launch traced here: 48.5 us
  Pallas kernels  47.9 us (98%)
  between operations  0.65 us (1%)
    pallas_call x1, Pallas kernels, local_step(): pl.pallas_call(functools.partial(_logits_kernel, (batch, draft, depth, vo...  27.3 us
    pallas_call x1, Pallas kernels, local_step(): pl.pallas_call(functools.partial(_verify_kernel, (batch, draft, vocab, nt...  14.8 us
    pallas_call x1, Pallas kernels, local_step(): pl.pallas_call(functools.partial(_write_kernel, (batch, draft, vocab)), o...  5.74 us

profile of v6, /device:TPU:81, one launch (start us, length us, event | category | flops | bytes accessed | tf_op | source)
XLA Modules:
  0.0 48.5 jit_solution(10113893798518683246)
XLA Ops:
  0.6 27.3 %logits.1 = (f32[126,256,128]{2,1,0:T(8,128)S(1)}, f32[126,256,128]{2,1,0:T(8,128)S(1)}, f32[320,128]{1,0:T(8,128)S(1)}, f32[320,128]{1,0:T(8,128)S(1)}, f32[1024,128]{1,0:T(8,128)S(1)}) custom-call(bf16[320,2048]{1,0:T(8,128)(2,1)} %bitcast.11, f32[1,2048]{1,0:T(1,128)} %bitcast.12, bf16[16032,2048]{1,0:T(8,128)(2,1)} %bitcast.10, f32[64,4,16032]{2,1,0:T(4,128)} %q_hbm.3, ...), custom_call_target="tpu_custom_call" | custom-call | tf_op jit(solution)/shard_map/logits/pallas_call | solution.py:492
  28.0 14.8 %verify.1 = (f32[126,256,128]{2,1,0:T(8,128)S(1)}, f32[256,128]{1,0:T(8,128)S(1)}, f32[256,128]{1,0:T(8,128)S(1)}, f32[4,64]{1,0:T(4,128)S(1)}, f32[4,128]{1,0:T(4,128)S(1)}, /*index=5*/f32[1,64]{1,0:T(1,128)S(1)}) custom-call(f32[126,256,128]{2,1,0:T(8,128)S(1)} %get-tuple-element.19.s_ref, ...), custom_call_target="tpu_custom_call", output_to_operand_aliasing={{0}: (1, {})} | custom-call | tf_op jit(solution)/shard_map/verify/pallas_call | solution.py:515
  42.8 5.7 %write.1 = (f32[64,4,16032]{2,1,0:T(4,128)}, f32[4,64]{1,0:T(4,128)}, f32[4,64]{1,0:T(4,128)}, f32[1,64]{1,0:T(1,128)}) custom-call(f32[126,256,128]{2,1,0:T(8,128)S(1)} %get-tuple-element.19.s_ref, f32[126,256,128]{2,1,0:T(8,128)S(1)} %get-tuple-element.24.q_ref, f32[256,128]{1,0:T(8,128)S(1)} %get-tuple-element.25.lse_ref, ...), custom_call_target="tpu_custom_call" | custom-call | tf_op jit(solution)/shard_map/write/pallas_call | solution.py:542

commit v7 on v6

--- a/solution.py
+++ b/solution.py
@@ -15,7 +15,7 @@
 CHUNK = 25
 W_PARTS = 2
 FENCES = 6
-Q_LATE = 4
+Q_LATE = 3
 TOK_STEP = 8
 SIG = (1, 3, 5, 7)
 GRP = {1: (0,), 3: (1, 2), 5: (3, 4)}
@@ -66,7 +66,7 @@
     def w_copy(n, i, size=part):
         slot = lax.rem(n, RING)
         return pltpu.make_async_copy(
-            w_hbm.at[pl.ds(n * STEP + i * part, size), :], w_buf.at[slot, pl.ds(i * part, size), :], w_sem.at[slot, i])
+            w_hbm.at[pl.ds(n * STEP + i * part, size), :], w_buf.at[slot, pl.ds(i * part, size), :], w_sem.at[slot])
 
     def w_wait(n):
         for i in range(W_PARTS):
@@ -190,7 +190,6 @@
                         online(g, q, c_old + q * (TILE // LANES), z, TILE // LANES,
                                None if penalty is None else [penalty] * (TILE // LANES))
 
-            pl.semaphore_wait(fence, len(SIG))
 
         w_wait(0)
         for q in range(2):
@@ -251,6 +250,7 @@
         for b in range(0, batch, 2):
             q_buf[nc - 1, pl.ds(b * draft, 2 * draft), pl.ds(0, last)] = jnp.concatenate([q_last[b], q_last[b + 1]], axis=0)
         fullstep(n, 0, lambda i: issue_late(n, i), next_full=False)
+        pl.semaphore_wait(fence, len(SIG) * full)
         for kk in range(half):
             for q in range(2):
                 for g in range(groups):
@@ -504,7 +504,7 @@
                 pltpu.VMEM((1, batch), f32),
                 pltpu.SMEM((draft, batch), jnp.int32),
                 dma,
-                dma((RING, W_PARTS)),
+                dma((RING,)),
                 dma((3,)),
                 dma((3,)),
                 pltpu.SemaphoreType.REGULAR,

time: 48.7 us -> 48.6 us (level)
  no operation moved by 1% of the time
where the time goes in v7:
time: 48.6 us; the launch traced here: 48.5 us
  Pallas kernels  47.9 us (99%)
  between operations  0.65 us (1%)
    pallas_call x1, Pallas kernels, local_step(): pl.pallas_call(functools.partial(_logits_kernel, (batch, draft, depth, vo...  27.3 us
    pallas_call x1, Pallas kernels, local_step(): pl.pallas_call(functools.partial(_verify_kernel, (batch, draft, vocab, nt...  14.8 us
    pallas_call x1, Pallas kernels, local_step(): pl.pallas_call(functools.partial(_write_kernel, (batch, draft, vocab)), o...  5.74 us

profile of v7, /device:TPU:81, one launch (start us, length us, event | category | flops | bytes accessed | tf_op | source)
XLA Modules:
  0.0 48.5 jit_solution(5813223960246086166)
XLA Ops:
  0.6 27.3 %logits.1 = (f32[126,256,128]{2,1,0:T(8,128)S(1)}, f32[126,256,128]{2,1,0:T(8,128)S(1)}, f32[320,128]{1,0:T(8,128)S(1)}, f32[320,128]{1,0:T(8,128)S(1)}, f32[1024,128]{1,0:T(8,128)S(1)}) custom-call(bf16[320,2048]{1,0:T(8,128)(2,1)} %bitcast.11, f32[1,2048]{1,0:T(1,128)} %bitcast.12, bf16[16032,2048]{1,0:T(8,128)(2,1)} %bitcast.10, f32[64,4,16032]{2,1,0:T(4,128)} %q_hbm.3, ...), custom_call_target="tpu_custom_call" | custom-call | tf_op jit(solution)/shard_map/logits/pallas_call | solution.py:492
  28.0 14.8 %verify.1 = (f32[126,256,128]{2,1,0:T(8,128)S(1)}, f32[256,128]{1,0:T(8,128)S(1)}, f32[256,128]{1,0:T(8,128)S(1)}, f32[4,64]{1,0:T(4,128)S(1)}, f32[4,128]{1,0:T(4,128)S(1)}, /*index=5*/f32[1,64]{1,0:T(1,128)S(1)}) custom-call(f32[126,256,128]{2,1,0:T(8,128)S(1)} %get-tuple-element.19.s_ref, ...), custom_call_target="tpu_custom_call", output_to_operand_aliasing={{0}: (1, {})} | custom-call | tf_op jit(solution)/shard_map/verify/pallas_call | solution.py:515
  42.8 5.7 %write.1 = (f32[64,4,16032]{2,1,0:T(4,128)}, f32[4,64]{1,0:T(4,128)}, f32[4,64]{1,0:T(4,128)}, f32[1,64]{1,0:T(1,128)}) custom-call(f32[126,256,128]{2,1,0:T(8,128)S(1)} %get-tuple-element.19.s_ref, f32[126,256,128]{2,1,0:T(8,128)S(1)} %get-tuple-element.24.q_ref, f32[256,128]{1,0:T(8,128)S(1)} %get-tuple-element.25.lse_ref, ...), custom_call_target="tpu_custom_call" | custom-call | tf_op jit(solution)/shard_map/write/pallas_call | solution.py:542
